TPU v7x, 32 devices: a 4x4x1 block of a 4x4x8 slice. The times are simulated.
32 devices in a mesh: dp: 1 (over z), ep: 32 (over y, x, core).
Axes of the slice: x: 4, y: 4, z: 1, core: 2. Of those that a mesh axis runs over, the one named last changes fastest.
The devices are a block of a 4x4x8 slice.
Arguments:
- x_in: bfloat16 [1024, 2048], P(('dp', 'ep'))
- k_cache: bfloat16 [1024, 32, 16, 128], P(('dp', 'ep'))
- v_cache: bfloat16 [1024, 32, 16, 128], P(('dp', 'ep'))
- cache_len: int32 [1024], P(('dp', 'ep'))
- topk_idx: int32 [1024, 8], P(('dp', 'ep'))
- ln_attn: bfloat16 [2048], replicated
- w_q: bfloat16 [2048, 2048], replicated
- w_k: bfloat16 [2048, 2048], replicated
- w_v: bfloat16 [2048, 2048], replicated
- q_norm: bfloat16 [128], replicated
- k_norm: bfloat16 [128], replicated
- w_o: bfloat16 [2048, 2048], replicated
- ln_moe: bfloat16 [2048], replicated
- w_router: bfloat16 [2048, 64], replicated
- w_gate: bfloat16 [64, 2048, 1024], P('ep')
- w_up: bfloat16 [64, 2048, 1024], P('ep')
- w_down: bfloat16 [64, 1024, 2048], P('ep')
Outputs:
- output 1: bfloat16 [1024, 2048], P(('dp', 'ep'))
- output 2: bfloat16 [1024, 32, 16, 128], P(('dp', 'ep'))
- output 3: bfloat16 [1024, 32, 16, 128], P(('dp', 'ep'))
All inputs are finite; a program needn't handle non-finite values.
Results may differ from a plain program's by a relative error of at most 0.0142719.
Values are sent between devices in bfloat16 or wider.
A program may use at most 768 MiB of HBM per device.

v0:
```python
import jax
import jax.numpy as jnp
from jax import lax
from jax.sharding import PartitionSpec as P

ROPE_BASE = 1000000.0
NORM_EPS = 1e-6


def norm_scale(values, gain_vec):
    return values * lax.rsqrt(jnp.mean(values * values, axis=-1, keepdims=True) + NORM_EPS) * gain_vec.astype(jnp.float32)


def rotate_halves(values, positions):
    half_dim = values.shape[-1] // 2
    freq_vec = ROPE_BASE ** (-jnp.arange(half_dim, dtype=jnp.float32) * 2.0 / values.shape[-1])
    angles = positions.astype(jnp.float32)[:, None, None] * freq_vec
    cosine = jnp.cos(angles)
    sine_val = jnp.sin(angles)
    lo_half = values[..., :half_dim]
    hi_half = values[..., half_dim:]
    return jnp.concatenate([lo_half * cosine - hi_half * sine_val, hi_half * cosine + lo_half * sine_val], axis=-1)


def attend_block(x_in, k_cache, v_cache, cache_len, ln_attn, w_q, w_k, w_v, q_norm, k_norm, w_o):
    n_batch, n_slots, kv_heads, head_dim = k_cache.shape
    q_heads = w_q.shape[1] // head_dim
    resid_in = x_in.astype(jnp.float32)
    normed = norm_scale(resid_in, ln_attn).astype(jnp.bfloat16)
    q_proj = jnp.dot(normed, w_q, preferred_element_type=jnp.float32).reshape(n_batch, q_heads, head_dim)
    k_proj = jnp.dot(normed, w_k, preferred_element_type=jnp.float32).reshape(n_batch, kv_heads, head_dim)
    v_new = jnp.dot(normed, w_v, preferred_element_type=jnp.float32).astype(jnp.bfloat16).reshape(n_batch, kv_heads, head_dim)
    q_rot = rotate_halves(norm_scale(q_proj, q_norm), cache_len).astype(jnp.bfloat16).reshape(n_batch, kv_heads, q_heads // kv_heads, head_dim)
    k_new = rotate_halves(norm_scale(k_proj, k_norm), cache_len).astype(jnp.bfloat16)
    len_col = cache_len[:, None, None, None]
    is_new = lax.broadcasted_iota(jnp.int32, (1, n_slots, 1, 1), 1) == len_col
    k_full = jnp.where(is_new, k_new[:, None], k_cache)
    v_full = jnp.where(is_new, v_new[:, None], v_cache)
    scores = jnp.einsum('bgrd,bsgd->bgrs', q_rot, k_full, preferred_element_type=jnp.float32) * head_dim ** -0.5
    seen = lax.broadcasted_iota(jnp.int32, (1, 1, 1, n_slots), 3) <= len_col
    attn_prob = jax.nn.softmax(jnp.where(seen, scores, -1e30), axis=-1).astype(jnp.bfloat16)
    attn_out = jnp.einsum('bgrs,bsgd->bgrd', attn_prob, v_full, preferred_element_type=jnp.float32).astype(jnp.bfloat16).reshape(n_batch, q_heads * head_dim)
    x_mid = (resid_in + jnp.dot(attn_out, w_o, preferred_element_type=jnp.float32)).astype(jnp.bfloat16)
    return x_mid, k_full, v_full


def route_gate(x_mid, ln_moe, w_router, topk_idx):
    resid_mid = x_mid.astype(jnp.float32)
    h_moe = norm_scale(resid_mid, ln_moe).astype(jnp.bfloat16)
    logits = jnp.dot(h_moe, w_router, preferred_element_type=jnp.float32)
    gate_wts = jax.nn.softmax(jnp.take_along_axis(logits, topk_idx, axis=1), axis=-1)
    return resid_mid, h_moe, gate_wts


def pack_rows(h_moe, topk_idx, ep_size, e_local, cap_rows):
    b_dev, top_k = topk_idx.shape
    pair_count = b_dev * top_k
    flat_idx = topk_idx.reshape(pair_count)
    dest_dev = flat_idx // e_local
    dest_hot = (dest_dev[:, None] == jnp.arange(ep_size)[None, :]).astype(jnp.int32)
    dev_counts = jnp.sum(dest_hot, axis=0)
    slot_rank = jnp.sum(jnp.cumsum(dest_hot, axis=0) * dest_hot, axis=1) - 1
    dev_start = jnp.cumsum(dev_counts) - dev_counts
    sort_order = jnp.argsort(dest_dev, stable=True)
    seat_ids = jnp.arange(cap_rows)
    pair_at = sort_order[jnp.minimum(dev_start[:, None] + seat_ids[None, :], pair_count - 1)]
    filled = seat_ids[None, :] < dev_counts[:, None]
    send_rows = jnp.where(filled[:, :, None], h_moe[pair_at // top_k], jnp.zeros((), jnp.bfloat16))
    send_ids = jnp.where(filled, (flat_idx % e_local)[pair_at], e_local - 1)
    return send_rows, send_ids, dest_dev * cap_rows + slot_rank


def group_count(row_ids, e_local):
    return jnp.sum((row_ids[:, None] == jnp.arange(e_local)[None, :]).astype(jnp.int32), axis=0)


def expert_sorted(sorted_rows, group_sizes, w_gate, w_up, w_down):
    gate_act = lax.ragged_dot(sorted_rows, w_gate, group_sizes, preferred_element_type=jnp.float32)
    up_act = lax.ragged_dot(sorted_rows, w_up, group_sizes, preferred_element_type=jnp.float32)
    hidden_act = (jax.nn.silu(gate_act) * up_act).astype(jnp.bfloat16)
    return lax.ragged_dot(hidden_act, w_down, group_sizes, preferred_element_type=jnp.float32).astype(jnp.bfloat16)


def expert_rows(tok_rows, row_ids, w_gate, w_up, w_down):
    sort_order = jnp.argsort(row_ids, stable=True)
    sorted_out = expert_sorted(tok_rows[sort_order], group_count(row_ids, w_gate.shape[0]), w_gate, w_up, w_down)
    return sorted_out[jnp.argsort(sort_order, stable=True)]


def unpack_rows(back_rows, flat_slot, gate_wts):
    b_dev, top_k = gate_wts.shape
    picked = back_rows[flat_slot].reshape(b_dev, top_k, back_rows.shape[1])
    return jnp.sum(picked.astype(jnp.float32) * gate_wts[:, :, None], axis=1)


def solution(mesh):
    ep_size = mesh.shape['ep']
    row_spec = P(('dp', 'ep'))
    replicated = P()
    expert_spec = P('ep')
    in_specs = (row_spec, row_spec, row_spec, row_spec, row_spec, replicated, replicated, replicated, replicated, replicated, replicated, replicated, replicated, replicated, expert_spec, expert_spec, expert_spec)
    out_specs = (row_spec, row_spec, row_spec)

    def device_step(x_in, k_cache, v_cache, cache_len, topk_idx, ln_attn, w_q, w_k, w_v, q_norm, k_norm, w_o, ln_moe, w_router, w_gate, w_up, w_down):
        x_mid, k_full, v_full = attend_block(x_in, k_cache, v_cache, cache_len, ln_attn, w_q, w_k, w_v, q_norm, k_norm, w_o)
        resid_mid, h_moe, gate_wts = route_gate(x_mid, ln_moe, w_router, topk_idx)
        b_dev, top_k = topk_idx.shape
        hidden = h_moe.shape[1]
        e_local = w_gate.shape[0]
        cap_rows = min(b_dev, 2 * b_dev * top_k // ep_size)
        send_rows, send_ids, flat_slot = pack_rows(h_moe, topk_idx, ep_size, e_local, cap_rows)
        recv_rows = lax.all_to_all(send_rows, 'ep', 0, 0, tiled=True).reshape(ep_size * cap_rows, hidden)
        recv_ids = lax.all_to_all(send_ids, 'ep', 0, 0, tiled=True).reshape(ep_size * cap_rows)
        expert_out = expert_rows(recv_rows, recv_ids, w_gate, w_up, w_down)
        back_rows = lax.all_to_all(expert_out.reshape(ep_size, cap_rows, hidden), 'ep', 0, 0, tiled=True).reshape(ep_size * cap_rows, hidden)
        moe_out = unpack_rows(back_rows, flat_slot, gate_wts)
        return (resid_mid + moe_out).astype(jnp.bfloat16), k_full, v_full

    return jax.shard_map(device_step, mesh=mesh, in_specs=in_specs, out_specs=out_specs, check_vma=False)
```

profile of v0, /device:TPU:97, one launch (start us, length us, event | category | flops | bytes accessed | tf_op | source)
XLA Modules:
  0.0 171.9 jit_solution(11198477024465653900)
XLA Ops:
  0.6 0.8 copy.39
  1.4 0.1 reshape.583
  1.5 0.1 reshape.575
  1.7 0.6 reduce-window.19
  2.3 0.2 slice_reduce_fusion
  2.5 3.2 %sort.48 = (s32[256]{0:T(256)}, s32[256]{0:T(256)S(1)}) sort(s32[256]{0:T(256)S(1)} %get-tuple-element.33, s32[256]{0:T(256)S(1)} %iota.61), dimensions={0}, to_apply=%region_7.8 | sort | flops 2048 | bytes 4096 | tf_op jit(solution)/shard_map/jit(argsort)/sort | solution.py:64
  5.7 0.1 fusion.27
  5.8 0.1 copy.40
  6.0 0.1 reduce.4
  6.3 3.5 %gather_fusion = s32[512]{0:T(512)S(1)} fusion(s32[256]{0:T(256)S(1)} %get-tuple-element.6, s32[1024]{0:T(1024)S(1)} %pad_clamp_fusion.5), kind=kCustom, calls=%fused_computation | custom fusion | bytes 6144 | tf_op jit(solution)/shard_map/gather | solution.py:66
  10.0 3.5 %gather_fusion.2 = s32[512]{0:T(512)S(1)} fusion(s32[256]{0:T(256)S(1)} %get-tuple-element.34, s32[1024]{0:T(1024)S(1)} %pad_clamp_fusion.4), kind=kCustom, calls=%fused_computation.2 | custom fusion | bytes 6144 | tf_op jit(solution)/shard_map/gather | solution.py:69
  13.6 0.7 fusion.31
  14.3 9.1 %all-to-all-start.1 = ((s32[32,1,16]{2,1,0:T(1,128)}), s32[32,1,16]{2,1,0:T(1,128)S(1)}, u32[]{:S(2)}, u32[]{:S(2)}) async-start(s32[32,1,16]{2,1,0:T(1,128)} %bitcast.7), calls=%async_computation.1 | async-start | bytes 32768 | tf_op jit(solution)/shard_map/all_to_all | solution.py:113
  23.7 0.1 fusion.15
  24.0 5.1 %fusion.13 = bf16[4,8,16,128]{3,1,2,0:T(8,128)(2,1)S(1)} fusion(bf16[2048,2048]{1,0:T(8,128)(2,1)} %param.25, bf16[32,2048]{1,0:T(8,128)(2,1)S(1)} %copy-done.3, f32[2048]{0:T(1024)S(1)} %convert_element_type.76, f32[32]{0:T(128)S(1)} %add_rsqrt_fusion.3), kind=kOutput, calls=%fused_computation.29 | convolution fusion | flops 268763136 | bytes 8659072 | tf_op jit(solution)/shard_map/dot_general | solution.py:32
  29.2 0.6 copy-done.1
  29.7 1.6 convolution_bitcast_fusion
  31.4 0.1 multiply_reduce_fusion.1
  31.6 0.7 slice-done.1
  32.3 1.6 convolution_bitcast_fusion.1
  34.0 0.1 multiply_reduce_fusion.2
  34.1 0.1 multiply_cosine_fusion
  34.3 0.2 multiply_multiply_fusion
  34.5 0.2 subtract_convert_fusion.1
  34.7 0.1 maximum_bitcast_fusion
  34.8 0.1 pad_maximum_fusion
  35.0 1.3 copy-done.4
  36.3 3.0 %broadcast_select_fusion.1 = (bf16[32,32,16,128]{3,2,1,0:T(8,128)(2,1)S(1)}, bf16[32,32,16,128]{3,2,1,0:T(8,128)(2,1)}) fusion(bf16[32,32,16,128]{3,2,1,0:T(8,128)(2,1)S(1)} %copy-done.4, pred[32,32]{1,0:T(8,128)(4,1)S(1)} %get-tuple-element.38, bf16[32,16,128]{2,1,0:T(8,128)(2,1)S(1)} %pad_maximum_fusion, bf16[32,32,16,128]{3,2,1,0:T(8,128)(2,1)S(1)} %copy-done.5, ...), kind=kLoop, calls=%fused_computation.14 | loop fusion | flops 4194304 | bytes 17040384 | tf_op jit(solution)/shard_map/jit(_where)/select_n | solution.py:37
  39.2 2.0 %copy-done.6 = bf16[32,32,16,128]{3,2,1,0:T(8,128)(2,1)} copy-done((bf16[32,32,16,128]{3,2,1,0:T(8,128)(2,1)}, bf16[32,32,16,128]{3,2,1,0:T(8,128)(2,1)S(1)}, u32[]{:S(2)}) %copy-start.6) | copy-done | bytes 4194328
  41.2 2.2 %fusion.4 = f32[32,16,1,32]{3,2,1,0:T(1,128)S(1)} fusion(bf16[32,32,16,128]{3,2,1,0:T(8,128)(2,1)S(1)} %get-tuple-element.31, bf16[32,16,128,1]{2,1,0,3:T(8,128)(2,1)S(1)} %maximum_bitcast_fusion), kind=kOutput, calls=%fused_computation.11 | convolution fusion | flops 4194304 | bytes 4390912 | tf_op jit(solution)/shard_map/bgrd,bsgd->bgrs/dot_general | solution.py:39
  43.5 0.3 fusion.14
  43.8 3.4 %fusion.2 = f32[32,16,1,128]{3,2,1,0:T(1,128)S(1)} fusion(bf16[32,32,16,128]{3,2,1,0:T(8,128)(2,1)} %get-tuple-element.32, bf16[32,16,32,1]{2,1,0,3:T(8,128)(2,1)S(1)} %fusion.14), kind=kOutput, calls=%fused_computation.9 | convolution fusion | flops 4194304 | bytes 4489216 | tf_op jit(solution)/shard_map/bgrs,bsgd->bgrd/dot_general | solution.py:42
  47.2 5.0 %multiply_reduce_fusion = (f32[32]{0:T(128)S(1)}, f32[32,2048]{1,0:T(8,128)S(1)}) fusion(bf16[2048,2048]{1,0:T(8,128)(2,1)} %param.28, bf16[4,8,16,128]{3,2,1,0:T(8,128)(2,1)S(1)} %bitcast.75, bf16[32,2048]{1,0:T(8,128)(2,1)S(1)} %copy-done.3), kind=kOutput, calls=%fused_computation.40 | convolution fusion | flops 268828640 | bytes 8913024 | tf_op jit(solution)/shard_map/dot_general | solution.py:43
  52.2 0.7 copy-done.7
  52.9 0.1 multiply_convert_fusion.1
  53.0 2.5 %gather_fusion.1 = bf16[512,2048]{1,0:T(8,128)(2,1)S(1)} fusion(bf16[32,2048]{1,0:T(8,128)(2,1)S(1)} %multiply_convert_fusion.1, s32[1024]{0:T(1024)S(1)} %pad_clamp_fusion.3), kind=kCustom, calls=%fused_computation.1 | custom fusion | bytes 4196352 | tf_op jit(solution)/shard_map/gather | solution.py:68
  55.5 1.6 broadcast_select_fusion.2
  57.1 6.3 %all-to-all-start = ((bf16[32,16,2048]{2,1,0:T(8,128)(2,1)}), bf16[32,16,2048]{2,1,0:T(8,128)(2,1)S(1)}, u32[]{:S(2)}, u32[]{:S(2)}) async-start(bf16[32,16,2048]{2,1,0:T(8,128)(2,1)} %broadcast_select_fusion.2), calls=%async_computation | async-start | bytes 4194304 | tf_op jit(solution)/shard_map/all_to_all | solution.py:112
  63.4 0.5 broadcast.587
  63.9 0.7 reduce.10
  64.7 3.8 %sort.49 = (s32[512]{0:T(512)}, s32[512]{0:T(512)S(1)}) sort(s32[512]{0:T(512)S(1)} %reshape.579, s32[512]{0:T(512)S(1)} %iota.62), dimensions={0}, to_apply=%region_9.10 | sort | flops 4608 | bytes 8192 | tf_op jit(solution)/shard_map/jit(argsort)/sort | solution.py:85
  68.5 0.6 fusion.34
  69.1 1.5 ragged-dot-metadata
  70.6 3.8 %sort.50 = (s32[512]{0:T(512)}, s32[512]{0:T(512)S(1)}) sort(s32[512]{0:T(512)S(1)} %get-tuple-element.7, s32[512]{0:T(512)S(1)} %iota.63), dimensions={0}, to_apply=%region_11.12 | sort | flops 4608 | bytes 8192 | tf_op jit(solution)/shard_map/jit(argsort)/sort | solution.py:87
  74.4 17.7 %all-to-all-done = bf16[32,16,2048]{2,1,0:T(8,128)(2,1)S(1)} async-done(((bf16[32,16,2048]{2,1,0:T(8,128)(2,1)}), bf16[32,16,2048]{2,1,0:T(8,128)(2,1)S(1)}, u32[]{:S(2)}, u32[]{:S(2)}) %all-to-all-start) | async-done | bytes 2097184 | tf_op jit(solution)/shard_map/all_to_all | solution.py:112
  92.1 3.3 %gather_fusion.3 = bf16[512,2048]{1,0:T(8,128)(2,1)} fusion(bf16[512,2048]{1,0:T(8,128)(2,1)S(1)} %bitcast.67, s32[1024]{0:T(1024)S(1)} %pad_clamp_fusion.2), kind=kCustom, calls=%fused_computation.3 | custom fusion | bytes 4196352 | tf_op jit(solution)/shard_map/gather | solution.py:86
  95.4 9.3 %ragged-dot-none.2 = f32[512,1024]{1,0:T(8,128)} custom-call(s32[1]{0:T(128)} %get-tuple-element.9, s32[3]{0:T(128)} %get-tuple-element.10, s32[3]{0:T(128)} %get-tuple-element.11, s32[3]{0:T(128)} %get-tuple-element.12, s32[1]{0:T(128)} %get-tuple-element.9, bf16[512,2048]{1,0:T(8,128)(2,1)} %gather_fusion.3, bf16[2,2048,1024]{2,1,0:T(8,128)(2,1)} %param.31), custom_call_target="tpu_custom_call" | custom-call | flops 2147483648 | bytes 12582920 | tf_op jit(solution)/shard_map/ragged_dot_general/ragged-dot-none
  104.7 9.5 %ragged-dot-none.1 = f32[512,1024]{1,0:T(8,128)} custom-call(s32[1]{0:T(128)} %get-tuple-element.9, s32[3]{0:T(128)} %get-tuple-element.10, s32[3]{0:T(128)} %get-tuple-element.11, s32[3]{0:T(128)} %get-tuple-element.12, s32[1]{0:T(128)} %get-tuple-element.9, bf16[512,2048]{1,0:T(8,128)(2,1)} %gather_fusion.3, bf16[2,2048,1024]{2,1,0:T(8,128)(2,1)} %param.32), custom_call_target="tpu_custom_call" | custom-call | flops 2147483648 | bytes 12582920 | tf_op jit(solution)/shard_map/ragged_dot_general/ragged-dot-none
  114.2 3.2 %multiply_convert_fusion = bf16[512,1024]{1,0:T(8,128)(2,1)} fusion(f32[512,1024]{1,0:T(8,128)} %ragged-dot-none.1, f32[512,1024]{1,0:T(8,128)S(1)} %copy-done.2), kind=kLoop, calls=%fused_computation.21 | loop fusion | flops 3145728 | bytes 5242880 | tf_op jit(solution)/shard_map/convert_element_type | solution.py:80
  117.4 9.5 %ragged-dot-none = f32[512,2048]{1,0:T(8,128)} custom-call(s32[1]{0:T(128)} %get-tuple-element.9, s32[3]{0:T(128)} %get-tuple-element.10, s32[3]{0:T(128)} %get-tuple-element.11, s32[3]{0:T(128)} %get-tuple-element.12, s32[1]{0:T(128)} %get-tuple-element.9, bf16[512,1024]{1,0:T(8,128)(2,1)} %multiply_convert_fusion, bf16[2,1024,2048]{2,1,0:T(8,128)(2,1)} %param.33), custom_call_target="tpu_custom_call" | custom-call | flops 2147483648 | bytes 13631496 | tf_op jit(solution)/shard_map/ragged_dot_general/ragged-dot-none
  126.9 2.5 %convert_element_type.91 = bf16[512,2048]{1,0:T(8,128)(2,1)S(1)} convert(f32[512,2048]{1,0:T(8,128)} %ragged-dot-none) | non-fusion elementwise | flops 1048576 | bytes 6291456 | tf_op jit(solution)/shard_map/convert_element_type | solution.py:81
  129.4 3.3 %gather_fusion.4 = bf16[512,2048]{1,0:T(8,128)(2,1)} fusion(bf16[512,2048]{1,0:T(8,128)(2,1)S(1)} %convert_element_type.91, s32[1024]{0:T(1024)S(1)} %pad_clamp_fusion.1), kind=kCustom, calls=%fused_computation.4 | custom fusion | bytes 4196352 | tf_op jit(solution)/shard_map/gather | solution.py:87
  132.7 6.4 %all-to-all-start.2 = ((bf16[32,16,2048]{2,1,0:T(8,128)(2,1)}), bf16[32,16,2048]{2,1,0:T(8,128)(2,1)S(1)}, u32[]{:S(2)}, u32[]{:S(2)}) async-start(bf16[32,16,2048]{2,1,0:T(8,128)(2,1)} %bitcast.71), calls=%async_computation.2 | async-start | bytes 4194304 | tf_op jit(solution)/shard_map/all_to_all | solution.py:115
  139.2 0.1 reshape.582
  139.3 0.1 reshape.635
  139.4 0.2 fusion.41
  139.5 2.0 %gather_fusion.6 = f32[256]{0:T(256)S(1)} fusion(f32[32,64]{1,0:T(8,128)S(1)} %fusion.41, s32[256]{0:T(256)S(1)} %reshape.635), kind=kCustom, calls=%fused_computation.6 | custom fusion | bytes 4096 | tf_op jit(solution)/shard_map/jit(take_along_axis)/gather | solution.py:51
  141.6 0.1 fusion.37
  141.8 0.2 fusion.33
  141.9 0.1 fusion.32
  142.0 25.8 %all-to-all-done.2 = bf16[32,16,2048]{2,1,0:T(8,128)(2,1)S(1)} async-done(((bf16[32,16,2048]{2,1,0:T(8,128)(2,1)}), bf16[32,16,2048]{2,1,0:T(8,128)(2,1)S(1)}, u32[]{:S(2)}, u32[]{:S(2)}) %all-to-all-start.2) | async-done | bytes 2097184 | tf_op jit(solution)/shard_map/all_to_all | solution.py:115
  167.9 1.4 gather_fusion.5
  169.2 1.0 fusion.8
  170.2 1.6 add_convert_fusion
  (73 shorter events, 1.3 us)
Async XLA Ops:
  0.6 138.7 %copy-start = (bf16[2048,64]{0,1:T(8,128)(2,1)S(1)}, bf16[2048,64]{0,1:T(8,128)(2,1)}, u32[]{:S(2)}) copy-start(bf16[2048,64]{0,1:T(8,128)(2,1)} %param.30) | copy-start | bytes 786436
  10.0 13.5 %copy-start.10 = (s32[32]{0:T(128)S(1)}, s32[32]{0:T(128)}, u32[]{:S(2)}) copy-start(s32[32]{0:T(128)} %param.20) | copy-start | bytes 388
  10.0 13.7 %copy-start.11 = (bf16[128]{0:T(256)(128)(2,1)S(1)}, bf16[128]{0:T(256)(128)(2,1)}, u32[]{:S(2)}) copy-start(bf16[128]{0:T(256)(128)(2,1)} %param.26) | copy-start | bytes 772
  10.0 13.7 %copy-start.12 = (bf16[128]{0:T(256)(128)(2,1)S(1)}, bf16[128]{0:T(256)(128)(2,1)}, u32[]{:S(2)}) copy-start(bf16[128]{0:T(256)(128)(2,1)} %param.27) | copy-start | bytes 772
  10.0 13.7 %copy-start.3 = (bf16[32,2048]{1,0:T(8,128)(2,1)S(1)}, bf16[32,2048]{1,0:T(8,128)(2,1)}, u32[]{:S(2)}) copy-start(bf16[32,2048]{1,0:T(8,128)(2,1)} %param.17) | copy-start | bytes 393220
  10.0 13.8 %copy-start.8 = (bf16[2048]{0:T(1024)(128)(2,1)S(1)}, bf16[2048]{0:T(1024)(128)(2,1)}, u32[]{:S(2)}) copy-start(bf16[2048]{0:T(1024)(128)(2,1)} %param.22) | copy-start | bytes 12292
  10.0 13.8 %copy-start.9 = (bf16[2048]{0:T(1024)(128)(2,1)S(1)}, bf16[2048]{0:T(1024)(128)(2,1)}, u32[]{:S(2)}) copy-start(bf16[2048]{0:T(1024)(128)(2,1)} %param.29) | copy-start | bytes 12292
  14.3 42.8 %all-to-all-start.1 = ((s32[32,1,16]{2,1,0:T(1,128)}), s32[32,1,16]{2,1,0:T(1,128)S(1)}, u32[]{:S(2)}, u32[]{:S(2)}) async-start(s32[32,1,16]{2,1,0:T(1,128)} %bitcast.7), calls=%async_computation.1 | async-start | bytes 32768 | tf_op jit(solution)/shard_map/all_to_all | solution.py:113
  24.0 5.8 %copy-start.1 = (bf16[2048,2048]{1,0:T(8,128)(2,1)S(1)}, bf16[2048,2048]{1,0:T(8,128)(2,1)}, u32[]{:S(2)}) copy-start(bf16[2048,2048]{1,0:T(8,128)(2,1)} %param.24) | copy-start | bytes 25165828
  24.0 7.6 %slice-start = ((s8[8388608]{0:T(1024)(128)(4,1)}), s8[4194304]{0:T(1024)(128)(4,1)S(1)}, s32[]{:S(2)}) async-start(s8[8388608]{0:T(1024)(128)(4,1)} %bitcast.69), calls=%async_computation.3 | async-start | bytes 8388608
  29.1 3.2 %slice-start.1 = ((s8[8388608]{0:T(1024)(128)(4,1)}), s8[4194304]{0:T(1024)(128)(4,1)S(1)}, s32[]{:S(2)}) async-start(s8[8388608]{0:T(1024)(128)(4,1)} %bitcast.69), calls=%async_computation.4 | async-start | bytes 8388608
  32.3 2.7 %copy-start.5 = (bf16[32,32,16,128]{3,2,1,0:T(8,128)(2,1)S(1)}, bf16[32,32,16,128]{3,2,1,0:T(8,128)(2,1)}, u32[]{:S(2)}) copy-start(bf16[32,32,16,128]{3,2,1,0:T(8,128)(2,1)} %param.19) | copy-start | bytes 12582916
  33.9 2.3 %copy-start.4 = (bf16[32,32,16,128]{3,2,1,0:T(8,128)(2,1)S(1)}, bf16[32,32,16,128]{3,2,1,0:T(8,128)(2,1)}, u32[]{:S(2)}) copy-start(bf16[32,32,16,128]{3,2,1,0:T(8,128)(2,1)} %param.18) | copy-start | bytes 12582916
  39.2 2.0 %copy-start.6 = (bf16[32,32,16,128]{3,2,1,0:T(8,128)(2,1)}, bf16[32,32,16,128]{3,2,1,0:T(8,128)(2,1)S(1)}, u32[]{:S(2)}) copy-start(bf16[32,32,16,128]{3,2,1,0:T(8,128)(2,1)S(1)} %get-tuple-element.31) | copy-start | bytes 12582916
  52.2 0.7 copy-start.7
  57.1 35.0 %all-to-all-start = ((bf16[32,16,2048]{2,1,0:T(8,128)(2,1)}), bf16[32,16,2048]{2,1,0:T(8,128)(2,1)S(1)}, u32[]{:S(2)}, u32[]{:S(2)}) async-start(bf16[32,16,2048]{2,1,0:T(8,128)(2,1)} %broadcast_select_fusion.2), calls=%async_computation | async-start | bytes 4194304 | tf_op jit(solution)/shard_map/all_to_all | solution.py:112
  104.7 9.5 %copy-start.2 = (f32[512,1024]{1,0:T(8,128)S(1)}, f32[512,1024]{1,0:T(8,128)}, u32[]{:S(2)}) copy-start(f32[512,1024]{1,0:T(8,128)} %ragged-dot-none.2) | copy-start | bytes 6291460
  132.7 35.1 %all-to-all-start.2 = ((bf16[32,16,2048]{2,1,0:T(8,128)(2,1)}), bf16[32,16,2048]{2,1,0:T(8,128)(2,1)S(1)}, u32[]{:S(2)}, u32[]{:S(2)}) async-start(bf16[32,16,2048]{2,1,0:T(8,128)(2,1)} %bitcast.71), calls=%async_computation.2 | async-start | bytes 4194304 | tf_op jit(solution)/shard_map/all_to_all | solution.py:115
where the time goes:
time: 173 us; the launch traced here: 172 us
  waiting for transfers between devices  43.6 us (25%)
  Pallas kernels  29.8 us (17%)
  other arithmetic  28.9 us (17%)
  local copies, waits for them, and re-layouts  27.4 us (16%)
  starting transfers between devices  21.9 us (13%)
  matrix products  19.2 us (11%)
    another operation x3, Pallas kernels  28.3 us
    all_to_all x1, waiting for transfers between devices, device_step(): lax.all_to_all(expert_out.reshape(ep_size, cap_rows, hidden), 'ep', 0, 0,...  25.8 us
    all_to_all x1, waiting for transfers between devices, device_step(): lax.all_to_all(send_rows, 'ep', 0, 0, tiled=True)  17.7 us
    all_to_all x1, starting transfers between devices, device_step(): lax.all_to_all(send_ids, 'ep', 0, 0, tiled=True).reshape(ep_size * cap_rows)  9.14 us
    all_to_all x1, starting transfers between devices, device_step(): lax.all_to_all(expert_out.reshape(ep_size, cap_rows, hidden), 'ep', 0, 0,...  6.42 us
    all_to_all x1, starting transfers between devices, device_step(): lax.all_to_all(send_rows, 'ep', 0, 0, tiled=True)  6.31 us
    unnamed x34, local copies, waits for them, and re-layouts  6.3 us
    dot_general x1, matrix products, attend_block(): jnp.dot(normed, w_v, preferred_element_type=jnp.float32)  5.13 us
  transfers between devices with their start and end apart: 3, of which 2 were waited for; matrix products, arithmetic and copies ran while one was open for 23% of the time, Pallas kernels for 1%

commit v1 on v0

v1 whole, which is shorter than its diff:
```python
import functools

import jax
import jax.numpy as jnp
from jax import lax
from jax.experimental import pallas as pl
from jax.experimental.pallas import tpu as pltpu
from jax.sharding import PartitionSpec as P

ROPE_BASE = 1000000.0
NORM_EPS = 1e-6
NEG = -1e30
RING = 4
CORES = 2
MESH = pl.DeviceIdType.MESH
F32 = jnp.float32
BF16 = jnp.bfloat16


def iota(shape, axis):
    return lax.broadcasted_iota(jnp.int32, shape, axis)


def split3(value):
    top = value.astype(BF16)
    rest = value - top.astype(F32)
    mid = rest.astype(BF16)
    low = (rest - mid.astype(F32)).astype(BF16)
    return top, mid, low


def dot32(lhs, rhs):
    return jnp.dot(lhs, rhs, preferred_element_type=F32)


def rms_rows(values, gain):
    return values * lax.rsqrt(jnp.mean(values * values, axis=-1, keepdims=True) + NORM_EPS) * gain


def route_rows(h_moe, topk, w_router, x_pos):
    rows, top_k = topk.shape
    experts = w_router.shape[1]
    e_local = experts // (RING * RING * CORES)
    devs = RING * RING * CORES
    seats = 2 * rows * top_k // devs
    logits = dot32(h_moe, w_router)
    expert_ids = iota((rows, experts), 1)
    hit = jnp.zeros((rows, experts), F32)
    for k in range(top_k):
        hit = hit + jnp.where(topk[:, k:k + 1] == expert_ids, 1.0, 0.0)
    chosen = hit > 0.5
    peak = jnp.max(jnp.where(chosen, logits, NEG), axis=1, keepdims=True)
    raw = jnp.where(chosen, jnp.exp(jnp.where(chosen, logits, peak) - peak), 0.0)
    gates = raw / jnp.sum(raw, axis=1, keepdims=True)
    hit_b = hit.astype(BF16)
    before = jnp.where(iota((rows, rows), 1) < iota((rows, rows), 0), 1.0, 0.0).astype(BF16)
    parts = split3(gates)
    lanes = devs * seats
    out = []
    for by_row in (True, False):
        lane_e = iota((experts, lanes), 1) // seats
        if by_row:
            lane_dev = lane_e
        else:
            lane_dev = (lane_e % (RING * CORES)) // CORES * (RING * CORES) + lane_e // (RING * CORES) * CORES + lane_e % CORES
        spread = jnp.where(iota((experts, lanes), 0) // e_local == lane_dev, 1.0, 0.0).astype(BF16)
        hit_l = dot32(hit_b, spread)
        rank_l = dot32(before, hit_l.astype(BF16))
        gate_l = dot32(parts[0], spread) + dot32(parts[1], spread) + dot32(parts[2], spread)
        seat_l = (iota((rows, lanes), 1) % seats).astype(F32)
        out.append(jnp.where(hit_l > 0.5, jnp.where(rank_l == seat_l, gate_l, 0.0), 0.0))
    place = jnp.where(iota((rows, 128), 1) == x_pos * rows + iota((rows, 128), 0), 1.0, 0.0).astype(BF16)
    marks = lax.dot_general((topk + 1).astype(F32).astype(BF16), place, (((0,), (0,)), ((), ())), preferred_element_type=F32)
    return out[0], out[1], marks


def norm_scale(values, gain_vec):
    return values * lax.rsqrt(jnp.mean(values * values, axis=-1, keepdims=True) + NORM_EPS) * gain_vec.astype(jnp.float32)


def rotate_halves(values, positions):
    half_dim = values.shape[-1] // 2
    freq_vec = ROPE_BASE ** (-jnp.arange(half_dim, dtype=jnp.float32) * 2.0 / values.shape[-1])
    angles = positions.astype(jnp.float32)[:, None, None] * freq_vec
    cosine = jnp.cos(angles)
    sine_val = jnp.sin(angles)
    lo_half = values[..., :half_dim]
    hi_half = values[..., half_dim:]
    return jnp.concatenate([lo_half * cosine - hi_half * sine_val, hi_half * cosine + lo_half * sine_val], axis=-1)


def attend_block(x_in, k_cache, v_cache, cache_len, ln_attn, w_q, w_k, w_v, q_norm, k_norm, w_o):
    n_batch, n_slots, kv_heads, head_dim = k_cache.shape
    q_heads = w_q.shape[1] // head_dim
    resid_in = x_in.astype(jnp.float32)
    normed = norm_scale(resid_in, ln_attn).astype(jnp.bfloat16)
    q_proj = jnp.dot(normed, w_q, preferred_element_type=jnp.float32).reshape(n_batch, q_heads, head_dim)
    k_proj = jnp.dot(normed, w_k, preferred_element_type=jnp.float32).reshape(n_batch, kv_heads, head_dim)
    v_new = jnp.dot(normed, w_v, preferred_element_type=jnp.float32).astype(jnp.bfloat16).reshape(n_batch, kv_heads, head_dim)
    q_rot = rotate_halves(norm_scale(q_proj, q_norm), cache_len).astype(jnp.bfloat16).reshape(n_batch, kv_heads, q_heads // kv_heads, head_dim)
    k_new = rotate_halves(norm_scale(k_proj, k_norm), cache_len).astype(jnp.bfloat16)
    len_col = cache_len[:, None, None, None]
    is_new = lax.broadcasted_iota(jnp.int32, (1, n_slots, 1, 1), 1) == len_col
    k_full = jnp.where(is_new, k_new[:, None], k_cache)
    v_full = jnp.where(is_new, v_new[:, None], v_cache)
    scores = jnp.einsum('bgrd,bsgd->bgrs', q_rot, k_full, preferred_element_type=jnp.float32) * head_dim ** -0.5
    seen = lax.broadcasted_iota(jnp.int32, (1, 1, 1, n_slots), 3) <= len_col
    attn_prob = jax.nn.softmax(jnp.where(seen, scores, -1e30), axis=-1).astype(jnp.bfloat16)
    attn_out = jnp.einsum('bgrs,bsgd->bgrd', attn_prob, v_full, preferred_element_type=jnp.float32).astype(jnp.bfloat16).reshape(n_batch, q_heads * head_dim)
    x_mid = (resid_in + jnp.dot(attn_out, w_o, preferred_element_type=jnp.float32)).astype(jnp.bfloat16)
    return x_mid, k_full, v_full


def route_kernel(x_mid, topk, ln_moe, w_router, h2, gate_a, gate_b, marks):
    h_moe = rms_rows(x_mid[...].astype(F32), ln_moe[...].astype(F32)).astype(BF16)
    h2[...] = h_moe
    x_pos = lax.axis_index('ep') // CORES % RING
    by_row, by_col, mark = route_rows(h_moe, topk[...], w_router[...], x_pos)
    for i in range(RING):
        gate_a[i] = by_row[:, i * 128:(i + 1) * 128]
        gate_b[i] = by_col[:, i * 128:(i + 1) * 128]
    marks[...] = mark


def route(x_mid, topk, ln_moe, w_router):
    rows, width = x_mid.shape
    return pl.pallas_call(
        route_kernel,
        out_shape=(jax.ShapeDtypeStruct((rows, width), BF16), jax.ShapeDtypeStruct((RING, rows, 128), F32), jax.ShapeDtypeStruct((RING, rows, 128), F32), jax.ShapeDtypeStruct((8, 128), F32)),
        name='route',
    )(x_mid, topk, ln_moe.reshape(1, width), w_router)


def exchange_kernel(h2, marks, gate_a, gate_b, x_mid, wg_hbm, wu_hbm, wd_hbm, out, hid, tok, gat_a, gat_b, wg, wu, wd, xs, ys, r1a, r1b, sa, sb, r2a, r2b,
                    w_sem, h_sem, t_sem, ga_sem, gb_sem, r1a_sem, r1b_sem, r2a_sem, r2b_sem, send_sem):
    rows, width = h2.shape
    half = width // 2
    seats = r1a.shape[2]
    ff = wg.shape[2]
    me = lax.axis_index('ep')
    c = me % CORES
    x = me // CORES % RING
    y = me // (CORES * RING)
    sends = []

    def dev(px, py, pc):
        return (py * RING + px) * CORES + pc

    def push(src, dst, sem, target):
        copy = pltpu.make_async_remote_copy(src_ref=src, dst_ref=dst, send_sem=send_sem.at[len(sends)], recv_sem=sem, device_id={'ep': target}, device_id_type=MESH)
        copy.start()
        sends.append(copy)

    def landed(ref, sem):
        pltpu.make_async_copy(ref, ref, sem).wait()

    def around(p, d):
        return (p + d) % RING

    other = 1 - c
    partner = dev(x, y, other)
    barrier = pltpu.get_barrier_semaphore()
    greet = [partner]
    for d in range(1, RING):
        greet += [dev(around(x, d), y, c), dev(around(x, d), y, other), dev(x, around(y, d), c), dev(x, around(y, d), other)]
    for target in greet:
        pl.semaphore_signal(barrier, inc=1, device_id={'ep': target}, device_id_type=MESH)

    loads = [pltpu.make_async_copy(s, d, w_sem.at[i]) for i, (s, d) in enumerate(((wg_hbm, wg), (wu_hbm, wu), (wd_hbm, wd)))]
    for load in loads:
        load.start()
    pl.semaphore_wait(barrier, len(greet))

    near = (1, 3, 2)
    own = [h2.at[:, pl.ds(0, half)], h2.at[:, pl.ds(half, half)]]

    def slot(part, py, pc, px):
        return hid.at[part, py, pc, px], h_sem.at[part, py, pc, px]

    for first in (True, False):
        for d in near:
            part_x, part_y = (0, 1) if first else (1, 0)
            push(own[part_x], *slot(part_x, y, c, x), dev(around(x, d), y, c))
            push(own[part_y], *slot(part_y, y, c, x), dev(x, around(y, d), c))
            if first:
                push(marks, tok.at[y, c, x], t_sem.at[y, c, x], dev(around(x, d), y, c))
                push(marks, tok.at[y, c, x], t_sem.at[y, c, x], dev(x, around(y, d), c))
        if first:
            push(own[0], *slot(0, y, c, x), partner)
            push(own[1], *slot(1, y, c, x), partner)
            push(marks, tok.at[y, c, x], t_sem.at[y, c, x], partner)
    for d in near:
        push(gate_b.at[around(x, d)], gat_b.at[x], gb_sem.at[x], dev(around(x, d), y, c))
        push(gate_a.at[around(y, d)], gat_a.at[y], ga_sem.at[y], dev(x, around(y, d), c))
    hid[0, y, c, x] = h2[:, :half]
    hid[1, y, c, x] = h2[:, half:]
    tok[y, c, x] = marks[...]
    gat_a[y] = gate_a[y]
    gat_b[x] = gate_b[x]

    late = []
    for d in near:
        px, py = around(x, d), around(y, d)
        for part, sy, sx in ((0, y, px), (1, py, x)):
            ref, sem = slot(part, sy, c, sx)
            landed(ref, sem)
            for e in near:
                target = dev(x, around(y, e), c) if part == 0 else dev(around(x, e), y, c)
                if e == 2:
                    late.append((ref, sem, target))
                else:
                    push(ref, ref, sem, target)
            push(ref, ref, sem, partner)
        ref, sem = tok.at[y, c, px], t_sem.at[y, c, px]
        landed(ref, sem)
        for e in near:
            push(ref, ref, sem, dev(x, around(y, e), c))
        push(ref, ref, sem, partner)
    for item in late:
        push(item[0], item[0], item[1], item[2])
    for d in near:
        px, py = around(x, d), around(y, d)
        for part, sy, sx in ((1, y, px), (0, py, x)):
            ref, sem = slot(part, sy, c, sx)
            landed(ref, sem)
            push(ref, ref, sem, partner)

    lane = iota((8, 128), 1)
    strict = jnp.where((iota((128, 128), 0) < iota((128, 128), 1)) & (iota((128, 128), 0) // rows == iota((128, 128), 1) // rows), 1.0, 0.0).astype(BF16)
    quad_seats = RING * seats

    def expert_chunk(step, py):
        keep = [[], []]
        for pc in range(CORES):
            ids = tok[py, pc, 0] + tok[py, pc, 1] + tok[py, pc, 2] + tok[py, pc, 3]
            hits = []
            for e in range(2):
                match = jnp.where(ids == (me * 2 + e + 1).astype(F32), 1.0, 0.0)
                hits.append(jnp.broadcast_to(jnp.sum(match, axis=0, keepdims=True), (8, 128)))
            rank = dot32((hits[0] + hits[1]).astype(BF16), strict)
            seat = rank + (lane // rows * seats).astype(F32)
            picks = []
            for e in range(2):
                pick = jnp.where((iota((quad_seats, 128), 0).astype(F32) == seat[0:1]) & (hits[e][0:1] > 0.5), 1.0, 0.0)
                keep[e].append(jnp.sum(pick, axis=1, keepdims=True))
                picks.append(pick.astype(BF16))
            pick = jnp.concatenate(picks, axis=0)
            for part in range(2):
                src = hid[part, py, pc].reshape(RING * rows, half)
                got = dot32(pick, src).astype(BF16)
                for e in range(2):
                    xs[e, pc * quad_seats:(pc + 1) * quad_seats, part * half:(part + 1) * half] = got[e * quad_seats:(e + 1) * quad_seats]
        if step == 0:
            loads[0].wait()
            loads[1].wait()
        hidden = []
        block = ff // 2
        for n in range(2):
            cols = slice(n * block, (n + 1) * block)
            a = dot32(xs[0], wg[0, :, cols]) + dot32(xs[1], wg[1, :, cols])
            u = dot32(xs[0], wu[0, :, cols]) + dot32(xs[1], wu[1, :, cols])
            hidden.append((jax.nn.silu(a) * u).astype(BF16))
        act = jnp.concatenate(hidden, axis=1)
        masks = [jnp.concatenate(k, axis=0) for k in keep]
        acts = [jnp.where(m > 0.5, act, jnp.zeros_like(act)) for m in masks]
        if step == 0:
            loads[2].wait()
        for n in range(4):
            cols = slice(n * half // 2, (n + 1) * half // 2)
            ys[step, :, cols] = (dot32(acts[0], wd[0, :, cols]) + dot32(acts[1], wd[1, :, cols])).astype(BF16)

    def first_leg(step, off):
        py = around(y, off)
        mine = CORES * x + c
        for dx in (0,) + near:
            for dc in range(CORES):
                px, pc = around(x, dx), (c + dc) % CORES
                src = ys.at[step, pl.ds((pc * RING + px) * seats, seats), pl.ds(0, half)]
                if dx == 0 and dc == 0:
                    r1a[py, mine] = src[...]
                else:
                    push(src, r1a.at[py, mine], r1a_sem.at[py, mine], dev(px, y, pc))
        for dc in range(CORES):
            pc = (c + dc) % CORES
            src = ys.at[step, pl.ds(pc * quad_seats, quad_seats), pl.ds(half, half)]
            if off == 0 and dc == 0:
                r1b[CORES * y + c] = src[...]
            else:
                push(src, r1b.at[CORES * y + c], r1b_sem.at[CORES * y + c], dev(x, py, pc))

    def weigh(gate, data):
        total = dot32(jnp.concatenate(split3(gate), axis=0), data)
        return total[:rows] + total[rows:2 * rows] + total[2 * rows:]

    def second_leg_a(off):
        py = around(y, off)
        for dx in (0,) + near:
            for dc in range(CORES):
                if dx or dc:
                    k = CORES * around(x, dx) + (c + dc) % CORES
                    landed(r1a.at[py, k], r1a_sem.at[py, k])
        if off:
            landed(gat_a.at[py], ga_sem.at[py])
        part = weigh(gat_a[py], r1a[py].reshape(RING * CORES * seats, half))
        if off:
            sa[py] = part
            push(sa.at[py], r2a.at[y], r2a_sem.at[y], dev(x, py, c))
        else:
            r2a[y] = part

    order = (0,) + near
    for step, off in enumerate(order):
        py = around(y, off)
        if step == 1:
            for d in near:
                qy = around(y, d)
                for e in near:
                    qx = around(x, e)
                    for part in range(2):
                        landed(*slot(part, qy, c, qx))
                        push(slot(part, qy, c, qx)[0], *slot(part, qy, c, qx), partner)
                for px in range(RING):
                    qx = around(x, px)
                    landed(tok.at[qy, c, qx], t_sem.at[qy, c, qx])
                    push(tok.at[qy, c, qx], tok.at[qy, c, qx], t_sem.at[qy, c, qx], partner)
        for px in range(RING):
            for part in range(2):
                landed(*slot(part, py, other, px))
            landed(tok.at[py, other, px], t_sem.at[py, other, px])
        expert_chunk(step, py)
        first_leg(step, off)
        if step:
            second_leg_a(order[step - 1])
    for d in near:
        for dc in range(CORES):
            k = CORES * around(y, d) + (c + dc) % CORES
            landed(r1b.at[k], r1b_sem.at[k])
    landed(r1b.at[CORES * y + other], r1b_sem.at[CORES * y + other])
    for d in near + (0,):
        px = around(x, d)
        if d:
            landed(gat_b.at[px], gb_sem.at[px])
        data = jnp.concatenate([r1b[k, pl.ds(px * seats, seats), :] for k in range(RING * CORES)], axis=0)
        part = weigh(gat_b[px], data)
        if d:
            sb[px] = part
            push(sb.at[px], r2b.at[x], r2b_sem.at[x], dev(px, y, c))
        else:
            r2b[x] = part
    second_leg_a(order[-1])
    for d in near:
        landed(r2a.at[around(y, d)], r2a_sem.at[around(y, d)])
    out[:, :half] = (x_mid[:, :half].astype(F32) + ((r2a[0] + r2a[1]) + (r2a[2] + r2a[3]))).astype(BF16)
    for d in near:
        landed(r2b.at[around(x, d)], r2b_sem.at[around(x, d)])
    out[:, half:] = (x_mid[:, half:].astype(F32) + ((r2b[0] + r2b[1]) + (r2b[2] + r2b[3]))).astype(BF16)
    for copy in sends:
        copy.wait_send()


def exchange(h2, marks, gate_a, gate_b, x_mid, w_gate, w_up, w_down, seats):
    rows, width = h2.shape
    half = width // 2
    e_local, _, ff = w_gate.shape
    line = RING * CORES
    vmem = pl.BlockSpec(memory_space=pltpu.VMEM)
    hbm = pl.BlockSpec(memory_space=pl.ANY)
    dma = pltpu.SemaphoreType.DMA
    return pl.pallas_call(
        exchange_kernel,
        out_shape=jax.ShapeDtypeStruct((rows, width), BF16),
        in_specs=[vmem] * 5 + [hbm] * 3,
        out_specs=vmem,
        scratch_shapes=[
            pltpu.VMEM((2, RING, CORES, RING, rows, half), BF16),
            pltpu.VMEM((RING, CORES, RING, 8, 128), F32),
            pltpu.VMEM((RING, rows, 128), F32),
            pltpu.VMEM((RING, rows, 128), F32),
            pltpu.VMEM(w_gate.shape, BF16),
            pltpu.VMEM(w_up.shape, BF16),
            pltpu.VMEM(w_down.shape, BF16),
            pltpu.VMEM((e_local, line * seats, width), BF16),
            pltpu.VMEM((RING, line * seats, width), BF16),
            pltpu.VMEM((RING, line, seats, half), BF16),
            pltpu.VMEM((line, RING * seats, half), BF16),
            pltpu.VMEM((RING, rows, half), F32),
            pltpu.VMEM((RING, rows, half), F32),
            pltpu.VMEM((RING, rows, half), F32),
            pltpu.VMEM((RING, rows, half), F32),
            dma((3,)),
            dma((2, RING, CORES, RING)),
            dma((RING, CORES, RING)),
            dma((RING,)),
            dma((RING,)),
            dma((RING, line)),
            dma((line,)),
            dma((RING,)),
            dma((RING,)),
            dma((192,)),
        ],
        compiler_params=pltpu.CompilerParams(collective_id=0, has_side_effects=True, vmem_limit_bytes=60 * 2 ** 20),
        name='exchange',
    )(h2, marks, gate_a, gate_b, x_mid, w_gate, w_up, w_down)


def solution(mesh):
    row_spec = P(('dp', 'ep'))
    rep = P()
    expert_spec = P('ep')
    in_specs = (row_spec,) * 5 + (rep,) * 9 + (expert_spec,) * 3

    def device_step(x_in, k_cache, v_cache, cache_len, topk_idx, ln_attn, w_q, w_k, w_v, q_norm, k_norm, w_o, ln_moe, w_router, w_gate, w_up, w_down):
        x_mid, k_full, v_full = attend_block(x_in, k_cache, v_cache, cache_len, ln_attn, w_q, w_k, w_v, q_norm, k_norm, w_o)
        rows, top_k = topk_idx.shape
        seats = 2 * rows * top_k // mesh.shape['ep']
        h2, gate_a, gate_b, marks = route(x_mid, topk_idx, ln_moe, w_router)
        x_out = exchange(h2, marks, gate_a, gate_b, x_mid, w_gate, w_up, w_down, seats)
        return x_out, k_full, v_full

    return jax.shard_map(device_step, mesh=mesh, in_specs=in_specs, out_specs=(row_spec,) * 3, check_vma=False)
```

time: 173 us -> 97.2 us (0.56)
  waiting for transfers between devices: 43.6 us -> 0 us
  Pallas kernels: 29.8 us -> 62 us
  other arithmetic: 28.9 us -> 6.79 us
  starting transfers between devices: 21.9 us -> 0 us
  local copies, waits for them, and re-layouts: 27.4 us -> 7.66 us
    pallas_call x0 -> x2, Pallas kernels: none -> 62 us  [the longest x1 59.4 us: exchange(): pl.pallas_call(exchange_kernel, out_shape=jax.ShapeDtypeStruct((rows, wid...]
    all_to_all x3 -> x0, waiting for transfers between devices: 43.6 us -> none  [the longest x1 25.8 us: device_step(): lax.all_to_all(expert_out.reshape(ep_size, cap_rows, hidden), 'ep', 0, 0,...]
    another operation x3 -> x0, Pallas kernels: 28.3 us -> none
    all_to_all x3 -> x0, starting transfers between devices: 21.9 us -> none  [the longest x1 9.14 us: device_step(): lax.all_to_all(send_ids, 'ep', 0, 0, tiled=True).reshape(ep_size * cap_rows)]
    gather x11 -> x0, local copies, waits for them, and re-layouts: 19.8 us -> none  [the longest x2 3.58 us: pack_rows(): sort_order[jnp.minimum(dev_start[:, None] + seat_ids[None, :], pair_count...]
    sort x3 -> x0, other arithmetic: 10.7 us -> none  [the longest x1 3.77 us: expert_rows(): sort_order = jnp.argsort(row_ids, stable=True)]
    convert_element_type x5 -> x0, other arithmetic: 7.41 us -> none  [the longest x1 3.17 us: expert_sorted(): hidden_act = (jax.nn.silu(gate_act) * up_act).astype(jnp.bfloat16)]
    dot_general x1, matrix products: 1.6 us -> 5.19 us  [attend_block(): jnp.dot(normed, w_k, preferred_element_type=jnp.float32)]
  transfers between devices with their start and end apart: 3 -> 0, of which waited for: 2 -> 0; matrix products, arithmetic and copies ran while one was open for 23% -> 0% of each run, Pallas kernels for 1% -> 0%
where the time goes in v1:
time: 97.2 us; the launch traced here: 97 us
  Pallas kernels  62 us (64%)
  matrix products  19.7 us (20%)
  local copies, waits for them, and re-layouts  7.66 us (8%)
  other arithmetic  6.79 us (7%)
    pallas_call x1, Pallas kernels, exchange(): pl.pallas_call(exchange_kernel, out_shape=jax.ShapeDtypeStruct((rows, wid...  59.4 us
    unnamed x34, local copies, waits for them, and re-layouts  7.06 us
    dot_general x1, matrix products, attend_block(): jnp.dot(attn_out, w_o, preferred_element_type=jnp.float32)  5.64 us
    dot_general x1, matrix products, attend_block(): jnp.dot(normed, w_k, preferred_element_type=jnp.float32)  5.19 us
    dot_general x1, matrix products, attend_block(): jnp.einsum('bgrs,bsgd->bgrd', attn_prob, v_full, preferred_element_type=j...  3.39 us
    select_n x1, other arithmetic, attend_block(): k_full = jnp.where(is_new, k_new[:, None], k_cache)  2.97 us
    pallas_call x1, Pallas kernels, route(): pl.pallas_call(route_kernel, out_shape=(jax.ShapeDtypeStruct((rows, width...  2.57 us
    dot_general x1, matrix products, attend_block(): jnp.einsum('bgrd,bsgd->bgrs', q_rot, k_full, preferred_element_type=jnp.f...  2.25 us

profile of v1, /device:TPU:97, one launch (start us, length us, event | category | flops | bytes accessed | tf_op | source)
XLA Modules:
  0.0 97.0 jit_solution(9509278208176589657)
XLA Ops:
  0.6 0.0 copy-start
  0.6 0.0 slice-start.2
  0.7 0.8 convert_element_type.42
  1.5 1.5 %fusion.13 = f32[32]{0:T(128)S(1)} fusion(bf16[32,2048]{1,0:T(8,128)(2,1)} %param.17), kind=kLoop, calls=%fused_computation.21 | loop fusion | flops 196576 | bytes 131200 | tf_op jit(solution)/shard_map/reduce_sum | solution.py:78
  3.0 0.0 slice-start.3
  3.0 5.2 %convolution_bitcast_fusion = f32[4,8,16,128]{3,1,2,0:T(8,128)S(1)} fusion(bf16[2048,2048]{1,0:T(8,128)(2,1)} %param.24, bf16[32,2048]{1,0:T(8,128)(2,1)} %param.17, f32[2048]{0:T(1024)S(1)} %convert_element_type.42, f32[32]{0:T(128)S(1)} %add_rsqrt_fusion.2), kind=kOutput, calls=%fused_computation.13 | convolution fusion | flops 268697600 | bytes 8790144 | tf_op jit(solution)/shard_map/dot_general | solution.py:98
  8.2 0.0 copy-start.8
  8.2 0.0 copy-start.9
  8.2 0.0 slice-start
  8.3 0.1 multiply_reduce_fusion
  8.5 0.0 copy-done
  8.5 0.0 slice-done.2
  8.5 0.0 slice-done.3
  8.5 0.0 copy-start.7
  8.5 0.0 slice-start.1
  8.5 1.6 %convolution_bitcast_fusion.1 = f32[4,8,16,128]{3,1,2,0:T(8,128)S(1)} fusion(bf16[2048,2048]{1,0:T(8,128)(2,1)S(1)} %bitcast.30, bf16[32,2048]{1,0:T(8,128)(2,1)S(1)} %copy-done, f32[2048]{0:T(1024)S(1)} %convert_element_type.42, f32[32]{0:T(128)S(1)} %add_rsqrt_fusion.2), kind=kOutput, calls=%fused_computation.14 | convolution fusion | flops 268697600 | bytes 8790144 | tf_op jit(solution)/shard_map/dot_general | solution.py:97
  10.1 0.1 copy.30
  10.2 0.1 multiply_reduce_fusion.1
  10.3 0.0 copy-done.8
  10.4 0.0 copy-done.9
  10.4 0.2 multiply_multiply_fusion
  10.6 0.0 copy-done.7
  10.6 0.1 multiply_cosine_fusion
  10.8 0.2 subtract_convert_fusion.1
  11.0 0.0 copy-start.1
  11.0 0.0 copy-start.2
  11.0 0.1 pad_maximum_fusion
  11.2 0.0 slice-done
  11.2 0.6 slice-done.1
  11.8 1.6 %fusion.11 = bf16[4,8,16,128]{3,1,2,0:T(8,128)(2,1)S(1)} fusion(bf16[2048,2048]{1,0:T(8,128)(2,1)S(1)} %bitcast.28, bf16[32,2048]{1,0:T(8,128)(2,1)S(1)} %copy-done, f32[2048]{0:T(1024)S(1)} %convert_element_type.42, f32[32]{0:T(128)S(1)} %add_rsqrt_fusion.2), kind=kOutput, calls=%fused_computation.17 | convolution fusion | flops 268763136 | bytes 8659072 | tf_op jit(solution)/shard_map/dot_general | solution.py:99
  13.4 0.1 iota_compare_fusion.1
  13.5 0.0 copy-done.1
  13.5 1.1 %copy-done.2 = bf16[32,32,16,128]{3,2,1,0:T(8,128)(2,1)S(1)} copy-done((bf16[32,32,16,128]{3,2,1,0:T(8,128)(2,1)S(1)}, bf16[32,32,16,128]{3,2,1,0:T(8,128)(2,1)}, u32[]{:S(2)}) %copy-start.2) | copy-done | bytes 4194328
  14.6 3.0 %broadcast_select_fusion.1 = (bf16[32,32,16,128]{3,2,1,0:T(8,128)(2,1)S(1)}, bf16[32,32,16,128]{3,2,1,0:T(8,128)(2,1)}) fusion(bf16[32,32,16,128]{3,2,1,0:T(8,128)(2,1)S(1)} %copy-done.1, pred[32,32]{1,0:T(8,128)(4,1)S(1)} %get-tuple-element.22, bf16[32,16,128]{2,1,0:T(8,128)(2,1)S(1)} %pad_maximum_fusion, bf16[32,32,16,128]{3,2,1,0:T(8,128)(2,1)S(1)} %copy-done.2, ...), kind=kLoop, calls=%fused_computation.7 | loop fusion | flops 4194304 | bytes 17040384 | tf_op jit(solution)/shard_map/jit(_where)/select_n | solution.py:104
  17.6 0.0 copy-start.3
  17.6 0.1 maximum_bitcast_fusion
  17.7 1.9 %copy-done.3 = bf16[32,32,16,128]{3,2,1,0:T(8,128)(2,1)} copy-done((bf16[32,32,16,128]{3,2,1,0:T(8,128)(2,1)}, bf16[32,32,16,128]{3,2,1,0:T(8,128)(2,1)S(1)}, u32[]{:S(2)}) %copy-start.3) | copy-done | bytes 4194328
  19.6 2.2 %fusion.4 = f32[32,16,1,32]{3,2,1,0:T(1,128)S(1)} fusion(bf16[32,32,16,128]{3,2,1,0:T(8,128)(2,1)S(1)} %get-tuple-element.29, bf16[32,16,128,1]{2,1,0,3:T(8,128)(2,1)S(1)} %maximum_bitcast_fusion), kind=kOutput, calls=%fused_computation.4 | convolution fusion | flops 4194304 | bytes 4390912 | tf_op jit(solution)/shard_map/bgrd,bsgd->bgrs/dot_general | solution.py:106
  21.8 0.3 fusion.12
  22.1 3.4 %fusion.2 = f32[32,16,1,128]{3,2,1,0:T(1,128)S(1)} fusion(bf16[32,32,16,128]{3,2,1,0:T(8,128)(2,1)} %get-tuple-element.30, bf16[32,16,32,1]{2,1,0,3:T(8,128)(2,1)S(1)} %fusion.12), kind=kOutput, calls=%fused_computation.2 | convolution fusion | flops 4194304 | bytes 4489216 | tf_op jit(solution)/shard_map/bgrs,bsgd->bgrd/dot_general | solution.py:109
  25.5 0.0 copy-start.4
  25.5 0.0 copy-start.5
  25.5 0.0 copy-start.6
  25.5 5.6 %fusion.6.x_mid = bf16[32,2048]{1,0:T(8,128)(2,1)} fusion(bf16[2048,2048]{1,0:T(8,128)(2,1)} %param.28, bf16[32,2048]{1,0:T(8,128)(2,1)S(1)} %copy-done, bf16[4,8,16,128]{3,2,1,0:T(8,128)(2,1)S(1)} %bitcast.33), kind=kOutput, calls=%fused_computation.9 | convolution fusion | flops 268632064 | bytes 8781824 | tf_op jit(solution)/shard_map/dot_general | solution.py:110
  31.2 0.0 copy-done.4
  31.2 1.0 %copy.23.w_router = bf16[2048,64]{1,0:T(8,128)(2,1)} copy(bf16[2048,64]{0,1:T(8,128)(2,1)S(1)} %copy-done.4) | data formatting | bytes 524288 | tf_op args[13]
  32.2 0.0 copy-done.5
  32.2 0.7 copy.22.topk
  32.9 0.0 copy-done.6
  32.9 0.6 reshape.201.ln_moe
  33.5 2.6 %route.1 = (bf16[32,2048]{1,0:T(8,128)(2,1)}, f32[4,32,128]{2,1,0:T(8,128)}, f32[4,32,128]{2,1,0:T(8,128)}, f32[8,128]{1,0:T(8,128)}) custom-call(bf16[32,2048]{1,0:T(8,128)(2,1)} %fusion.6.x_mid, s32[32,8]{1,0:T(8,128)} %copy.22.topk, bf16[1,2048]{1,0:T(2,128)(2,1)} %reshape.201.ln_moe, bf16[2048,64]{1,0:T(8,128)(2,1)} %copy.23.w_router), custom_call_target="tpu_custom_call" | custom-call | tf_op jit(solution)/shard_map/route/pallas_call | solution.py:127
  36.0 59.4 %exchange.1 = bf16[32,2048]{1,0:T(8,128)(2,1)} custom-call(bf16[32,2048]{1,0:T(8,128)(2,1)} %get-tuple-element.7.h2, f32[8,128]{1,0:T(8,128)} %get-tuple-element.8.marks, f32[4,32,128]{2,1,0:T(8,128)} %get-tuple-element.9.gate_a, f32[4,32,128]{2,1,0:T(8,128)} %get-tuple-element.10.gate_b, bf16[32,2048]{1,0:T(8,128)(2,1)} %fusion.6.x_mid, ...), custom_call_target="tpu_custom_call" | custom-call | tf_op jit(solution)/shard_map/exchange/pallas_call | solution.py:369
  95.5 1.6 %copy.47 = bf16[32,2048]{1,0:T(8,128)(2,1)} copy(bf16[32,2048]{1,0:T(8,128)(2,1)} %exchange.1) | data formatting | bytes 262144
  (12 shorter events, 0.1 us)
Async XLA Ops:
  0.6 7.8 %copy-start = (bf16[32,2048]{1,0:T(8,128)(2,1)S(1)}, bf16[32,2048]{1,0:T(8,128)(2,1)}, u32[]{:S(2)}) copy-start(bf16[32,2048]{1,0:T(8,128)(2,1)} %param.17) | copy-start | bytes 393220
  0.6 7.8 %slice-start.2 = ((s8[8388608]{0:T(1024)(128)(4,1)}), s8[4194304]{0:T(1024)(128)(4,1)S(1)}, s32[]{:S(2)}) async-start(s8[8388608]{0:T(1024)(128)(4,1)} %bitcast.29), calls=%async_computation.2 | async-start | bytes 8388608
  3.0 5.5 %slice-start.3 = ((s8[8388608]{0:T(1024)(128)(4,1)}), s8[4194304]{0:T(1024)(128)(4,1)S(1)}, s32[]{:S(2)}) async-start(s8[8388608]{0:T(1024)(128)(4,1)} %bitcast.29), calls=%async_computation.3 | async-start | bytes 8388608
  8.2 2.1 %copy-start.8 = (bf16[128]{0:T(256)(128)(2,1)S(1)}, bf16[128]{0:T(256)(128)(2,1)}, u32[]{:S(2)}) copy-start(bf16[128]{0:T(256)(128)(2,1)} %param.26) | copy-start | bytes 772
  8.2 2.2 %copy-start.9 = (bf16[128]{0:T(256)(128)(2,1)S(1)}, bf16[128]{0:T(256)(128)(2,1)}, u32[]{:S(2)}) copy-start(bf16[128]{0:T(256)(128)(2,1)} %param.27) | copy-start | bytes 772
  8.2 2.9 %slice-start = ((s8[8388608]{0:T(1024)(128)(4,1)}), s8[4194304]{0:T(1024)(128)(4,1)S(1)}, s32[]{:S(2)}) async-start(s8[8388608]{0:T(1024)(128)(4,1)} %bitcast.27), calls=%async_computation | async-start | bytes 8388608
  8.5 2.1 %copy-start.7 = (s32[32]{0:T(128)S(1)}, s32[32]{0:T(128)}, u32[]{:S(2)}) copy-start(s32[32]{0:T(128)} %param.20) | copy-start | bytes 388
  8.5 3.3 %slice-start.1 = ((s8[8388608]{0:T(1024)(128)(4,1)}), s8[4194304]{0:T(1024)(128)(4,1)S(1)}, s32[]{:S(2)}) async-start(s8[8388608]{0:T(1024)(128)(4,1)} %bitcast.27), calls=%async_computation.1 | async-start | bytes 8388608
  11.0 2.5 %copy-start.1 = (bf16[32,32,16,128]{3,2,1,0:T(8,128)(2,1)S(1)}, bf16[32,32,16,128]{3,2,1,0:T(8,128)(2,1)}, u32[]{:S(2)}) copy-start(bf16[32,32,16,128]{3,2,1,0:T(8,128)(2,1)} %param.18) | copy-start | bytes 12582916
  11.0 3.6 %copy-start.2 = (bf16[32,32,16,128]{3,2,1,0:T(8,128)(2,1)S(1)}, bf16[32,32,16,128]{3,2,1,0:T(8,128)(2,1)}, u32[]{:S(2)}) copy-start(bf16[32,32,16,128]{3,2,1,0:T(8,128)(2,1)} %param.19) | copy-start | bytes 12582916
  17.6 2.0 %copy-start.3 = (bf16[32,32,16,128]{3,2,1,0:T(8,128)(2,1)}, bf16[32,32,16,128]{3,2,1,0:T(8,128)(2,1)S(1)}, u32[]{:S(2)}) copy-start(bf16[32,32,16,128]{3,2,1,0:T(8,128)(2,1)S(1)} %get-tuple-element.29) | copy-start | bytes 12582916
  25.5 5.7 %copy-start.4 = (bf16[2048,64]{0,1:T(8,128)(2,1)S(1)}, bf16[2048,64]{0,1:T(8,128)(2,1)}, u32[]{:S(2)}) copy-start(bf16[2048,64]{0,1:T(8,128)(2,1)} %param.30) | copy-start | bytes 786436
  25.5 6.7 %copy-start.5 = (s32[32,8]{0,1:T(8,128)S(1)}, s32[32,8]{0,1:T(8,128)}, u32[]{:S(2)}) copy-start(s32[32,8]{0,1:T(8,128)} %param.21) | copy-start | bytes 3076
  25.5 7.3 %copy-start.6 = (bf16[2048]{0:T(1024)(128)(2,1)S(1)}, bf16[2048]{0:T(1024)(128)(2,1)}, u32[]{:S(2)}) copy-start(bf16[2048]{0:T(1024)(128)(2,1)} %param.29) | copy-start | bytes 12292

commit v2 on v1

v2 whole, which is shorter than its diff:
```python
import functools
import math

import jax
import jax.numpy as jnp
from jax import lax
from jax.experimental import pallas as pl
from jax.experimental.pallas import tpu as pltpu
from jax.sharding import PartitionSpec as P

ROPE_BASE = 1000000.0
NORM_EPS = 1e-6
NEG = -1e30
RING = 4
CORES = 2
MESH = pl.DeviceIdType.MESH
F32 = jnp.float32
BF16 = jnp.bfloat16


def iota(shape, axis):
    return lax.broadcasted_iota(jnp.int32, shape, axis)


def split3(value):
    top = value.astype(BF16)
    rest = value - top.astype(F32)
    mid = rest.astype(BF16)
    low = (rest - mid.astype(F32)).astype(BF16)
    return top, mid, low


def dot32(lhs, rhs):
    return jnp.dot(lhs, rhs, preferred_element_type=F32)


def rms_rows(values, gain):
    return values * lax.rsqrt(jnp.mean(values * values, axis=-1, keepdims=True) + NORM_EPS) * gain


def choice_tables(topk_t, experts, x_pos):
    top_k, rows = topk_t.shape
    devs = RING * RING * CORES
    e_local = experts // devs
    seats = 2 * rows * top_k // devs
    lanes = devs * seats
    topk_b = (topk_t + 1).astype(F32).astype(BF16)
    eye = jnp.where(iota((top_k, 128), 0) == iota((top_k, 128), 1), 1.0, 0.0).astype(BF16)
    topk = lax.dot_general(topk_b, eye, (((0,), (0,)), ((), ())), preferred_element_type=F32)
    expert_ids = (iota((rows, experts), 1) + 1).astype(F32)
    hit = jnp.zeros((rows, experts), F32)
    for k in range(top_k):
        hit = hit + jnp.where(topk[:, k:k + 1] == expert_ids, 1.0, 0.0)
    before = jnp.where(iota((rows, rows), 1) < iota((rows, rows), 0), 1.0, 0.0).astype(BF16)
    seat_l = (iota((rows, lanes), 1) % seats).astype(F32)
    tables = []
    for by_row in (True, False):
        hit_l = dot32(hit.astype(BF16), spread_matrix(experts, lanes, seats, e_local, by_row))
        rank_l = dot32(before, hit_l.astype(BF16))
        tables.append(jnp.where(rank_l == seat_l, hit_l, 0.0))
    place = jnp.where(iota((rows, 128), 1) == x_pos * rows + iota((rows, 128), 0), 1.0, 0.0).astype(BF16)
    return hit, tables[0], tables[1], dot32(topk_b, place)


def flat_row(value):
    return jnp.concatenate([value[i:i + 1] for i in range(value.shape[0])], axis=1)


def spread_matrix(experts, lanes, seats, e_local, by_row):
    lane_dev = iota((experts, lanes), 1) // seats
    if not by_row:
        lane_dev = (lane_dev % (RING * CORES)) // CORES * (RING * CORES) + lane_dev // (RING * CORES) * CORES + lane_dev % CORES
    return jnp.where(iota((experts, lanes), 0) // e_local == lane_dev, 1.0, 0.0).astype(BF16)


def attend_kernel(lens, x_in, topk_t, ln_attn, q_norm, k_norm, ln_moe, w_router_t, k_hbm, v_hbm, wq_hbm, wk_hbm, wv_hbm, wo_hbm,
                  k_out, v_out, x_mid, h2, gate_a, gate_b, marks, kbuf, vbuf, wq, wk, wv, wo, raw, q_s, k_s, v_s, o_s, xm_s, hit_s, tab_a, tab_b,
                  w_sem, c_sem, out_sem):
    rows, width = x_in.shape
    slots, heads, hd = kbuf.shape[1:]
    experts = w_router_t.shape[0]
    blk = 2 * hd
    n_blk = width // blk
    group = 8
    n_grp = rows // group
    ahead = 4

    def w_copy(i, which):
        src, dst = ((wq_hbm, wq), (wk_hbm, wk), (wv_hbm, wv), (wo_hbm, wo))[which]
        return pltpu.make_async_copy(src.at[:, pl.ds(pl.multiple_of(i * blk, blk), blk)], dst.at[i], w_sem.at[which, i])

    def c_copy(g, which):
        src, dst = ((k_hbm, kbuf), (v_hbm, vbuf))[which]
        return pltpu.make_async_copy(src.at[pl.ds(g * group, group)], dst.at[pl.ds(g * group, group)], c_sem.at[which, g])

    def o_copy(g, which):
        src, dst = ((kbuf, k_out), (vbuf, v_out))[which]
        return pltpu.make_async_copy(src.at[pl.ds(g * group, group)], dst.at[pl.ds(g * group, group)], out_sem.at[which, g])

    for i in range(ahead):
        for which in range(3):
            w_copy(i, which).start()

    hit, one, two, mark = choice_tables(topk_t[...], experts, lax.axis_index('ep') // CORES % RING)
    hit_s[...] = hit
    tab_a[...] = one
    tab_b[...] = two
    marks[...] = mark

    row = iota((rows, hd), 0)
    lane = iota((rows, hd), 1)
    pos = jnp.zeros((rows, hd), F32)
    for b in range(rows):
        pos = jnp.where(row == b, lens[b].astype(F32), pos)
    half = hd // 2
    freq = jnp.exp((lane % half).astype(F32) * (-2.0 * math.log(ROPE_BASE) / hd))
    cosine = jnp.cos(pos * freq)
    sine = jnp.where(lane < half, -1.0, 1.0) * jnp.sin(pos * freq)
    q_gain = jnp.broadcast_to(q_norm[...].astype(F32), (rows, hd))
    k_gain = jnp.broadcast_to(k_norm[...].astype(F32), (rows, hd))
    normed = rms_rows(x_in[...].astype(F32), flat_row(ln_attn[...].astype(F32))).astype(BF16)

    def turn(value, gain):
        value = rms_rows(value, gain)
        return value * cosine + pltpu.roll(value, half, 1) * sine

    later = [functools.partial(c_copy, g, which) for g in range(n_grp) for which in range(2)] + [functools.partial(w_copy, i, 3) for i in range(n_blk)]
    for i in range(n_blk + 1):
        if i + ahead < n_blk:
            for which in range(3):
                w_copy(i + ahead, which).start()
        elif later:
            for copy in later[:4]:
                copy().start()
            later = later[4:]
        if i < n_blk:
            for which, buf in enumerate((wq, wk, wv)):
                w_copy(i, which).wait()
            for which, buf in enumerate((wq, wk, wv)):
                raw[i % 2, which] = dot32(normed, buf[i])
        if i:
            for s in range(2):
                dst = pl.ds(2 * (i - 1) + s, rows, stride=heads)
                cols = slice(s * hd, (s + 1) * hd)
                q_s[dst, :] = turn(raw[(i - 1) % 2, 0, :, cols], q_gain)
                k_s[dst, :] = turn(raw[(i - 1) % 2, 1, :, cols], k_gain)
                v_s[dst, :] = raw[(i - 1) % 2, 2, :, cols]
    for copy in later:
        copy().start()

    key = iota((heads, slots * heads), 1)
    same = key % heads == iota((heads, slots * heads), 0)
    scale = hd ** -0.5

    def one_group(g, carry):
        c_copy(g, 0).wait()
        c_copy(g, 1).wait()
        scores = []
        for i in range(group):
            b = g * group + i
            at = pl.ds(pl.multiple_of(b * heads, heads), heads)
            length = lens[b]
            k_row = k_s[at, :].astype(BF16)
            v_row = v_s[at, :].astype(BF16)
            kbuf[b, length] = k_row
            vbuf[b, length] = v_row
            keys = kbuf[b].reshape(slots * heads, hd)
            score = lax.dot_general(q_s[at, :].astype(BF16), keys, (((1,), (1,)), ((), ())), preferred_element_type=F32) * scale
            scores.append(jnp.where(same & (key // heads <= length), score, NEG))
        for i in range(group):
            b = g * group + i
            raw = jnp.exp(scores[i] - jnp.max(scores[i], axis=1, keepdims=True))
            prob = (raw / jnp.sum(raw, axis=1, keepdims=True)).astype(BF16)
            mixed = dot32(prob, vbuf[b].reshape(slots * heads, hd))
            o_s[pl.ds(pl.multiple_of(b * heads, heads), heads), :] = mixed
        return carry

    lax.fori_loop(0, n_grp, one_group, 0)
    att = jnp.concatenate([o_s[pl.ds(h, rows, stride=heads), :].astype(BF16) for h in range(heads)], axis=1)
    for i in range(n_blk):
        w_copy(i, 3).wait()
        if i >= n_blk - n_grp:
            o_copy(i - n_blk + n_grp, 0).start()
            o_copy(i - n_blk + n_grp, 1).start()
        cols = slice(i * blk, (i + 1) * blk)
        xm_s[:, cols] = (x_in[:, cols].astype(F32) + dot32(att, wo[i])).astype(BF16)
    mid = xm_s[...]
    x_mid[...] = mid
    h_moe = rms_rows(mid.astype(F32), flat_row(ln_moe[...].astype(F32))).astype(BF16)
    h2[...] = h_moe
    logits = lax.dot_general(h_moe, w_router_t[...], (((1,), (1,)), ((), ())), preferred_element_type=F32)
    chosen = hit_s[...] > 0.5
    peak = jnp.max(jnp.where(chosen, logits, NEG), axis=1, keepdims=True)
    raw = jnp.where(chosen, jnp.exp(jnp.where(chosen, logits, peak) - peak), 0.0)
    parts = split3(raw / jnp.sum(raw, axis=1, keepdims=True))
    lanes = tab_a.shape[1]
    devs = RING * RING * CORES
    for by_row, table, dst in ((True, tab_a, gate_a), (False, tab_b, gate_b)):
        spread = spread_matrix(experts, lanes, lanes // devs, experts // devs, by_row)
        gate = (dot32(parts[0], spread) + dot32(parts[1], spread) + dot32(parts[2], spread)) * table[...]
        for i in range(RING):
            dst[i] = gate[:, i * 128:(i + 1) * 128]
    for g in range(n_grp):
        o_copy(g, 0).wait()
        o_copy(g, 1).wait()


def attend(x_in, k_cache, v_cache, cache_len, topk, ln_attn, w_q, w_k, w_v, q_norm, k_norm, w_o, ln_moe, w_router):
    rows, slots, heads, hd = k_cache.shape
    width = x_in.shape[1]
    experts = w_router.shape[1]
    lanes = 2 * rows * topk.shape[1]
    n_blk = width // (2 * hd)
    vmem = pl.BlockSpec(memory_space=pltpu.VMEM)
    hbm = pl.BlockSpec(memory_space=pl.ANY)
    dma = pltpu.SemaphoreType.DMA
    weight = pltpu.VMEM((n_blk, width, 2 * hd), BF16)
    return pl.pallas_call(
        attend_kernel,
        out_shape=(
            jax.ShapeDtypeStruct(k_cache.shape, BF16),
            jax.ShapeDtypeStruct(v_cache.shape, BF16),
            jax.ShapeDtypeStruct((rows, width), BF16),
            jax.ShapeDtypeStruct((rows, width), BF16),
            jax.ShapeDtypeStruct((RING, rows, 128), F32),
            jax.ShapeDtypeStruct((RING, rows, 128), F32),
            jax.ShapeDtypeStruct((8, 128), F32),
        ),
        in_specs=[pl.BlockSpec(memory_space=pltpu.SMEM)] + [vmem] * 7 + [hbm] * 6,
        out_specs=[hbm, hbm] + [vmem] * 5,
        scratch_shapes=[
            pltpu.VMEM(k_cache.shape, BF16),
            pltpu.VMEM(v_cache.shape, BF16),
            weight, weight, weight, weight,
            pltpu.VMEM((2, 3, rows, 2 * hd), F32),
            pltpu.VMEM((rows * heads, hd), F32),
            pltpu.VMEM((rows * heads, hd), F32),
            pltpu.VMEM((rows * heads, hd), F32),
            pltpu.VMEM((rows * heads, hd), F32),
            pltpu.VMEM((rows, width), BF16),
            pltpu.VMEM((rows, experts), F32),
            pltpu.VMEM((rows, lanes), F32),
            pltpu.VMEM((rows, lanes), F32),
            dma((4, n_blk)),
            dma((2, rows // 8)),
            dma((2, rows // 8)),
        ],
        compiler_params=pltpu.CompilerParams(vmem_limit_bytes=60 * 2 ** 20),
        name='attend',
    )(cache_len, x_in, topk.T, ln_attn.reshape(width // 128, 128), q_norm.reshape(1, hd), k_norm.reshape(1, hd), ln_moe.reshape(width // 128, 128), w_router.T, k_cache, v_cache, w_q, w_k, w_v, w_o)


def exchange_kernel(h2, marks, gate_a, gate_b, x_mid, wg_hbm, wu_hbm, wd_hbm, out, hid, tok, gat, wg, wu, wd, xs, ys, r1a, r1b, sa, sb, r2a, r2b,
                    w_sem, h_sem, hp_sem, t_sem, tp_sem, g_sem, r1a_sem, r1b_sem, r2_sem, send_sem):
    rows, width = h2.shape
    half = width // 2
    cut = r1a.shape[2]
    rest = width - cut
    seats = r1a.shape[1]
    ff = wg.shape[2]
    me = lax.axis_index('ep')
    c = me % CORES
    x = me // CORES % RING
    y = me // (CORES * RING)
    sent = [0] * 8

    def dev(px, py, pc):
        return (py * RING + px) * CORES + pc

    def push(kind, src, dst, sem, target):
        pltpu.make_async_remote_copy(src_ref=src, dst_ref=dst, send_sem=send_sem.at[kind], recv_sem=sem, device_id={'ep': target}, device_id_type=MESH).start()
        sent[kind] += 1

    def landed(ref, sem):
        pltpu.make_async_copy(ref, ref, sem).wait()

    def around(p, d):
        return (p + d) % RING

    other = 1 - c
    partner = dev(x, y, other)
    barrier = pltpu.get_barrier_semaphore()
    greet = [partner]
    for d in range(1, RING):
        greet += [dev(around(x, d), y, c), dev(around(x, d), y, other), dev(x, around(y, d), c), dev(x, around(y, d), other)]
    for target in greet:
        pl.semaphore_signal(barrier, inc=1, device_id={'ep': target}, device_id_type=MESH)

    loads = [pltpu.make_async_copy(s, d, w_sem.at[i]) for i, (s, d) in enumerate(((wg_hbm, wg), (wu_hbm, wu), (wd_hbm, wd)))]
    for load in loads:
        load.start()
    pl.semaphore_wait(barrier, len(greet))

    near = (1, 3, 2)

    def block_at(part, py, pc, px):
        return ((part * RING + py) * CORES + pc) * RING + px

    def slot(part, py, px):
        return hid.at[block_at(part, py, c, px)], h_sem.at[part, py, px]

    def mark_at(py, pc, px):
        return (py * CORES + pc) * RING + px

    def to_partner(part, py, px):
        ref = hid.at[block_at(part, py, c, px)]
        push(0, ref, ref, hp_sem.at[part, py], partner)

    own = [h2.at[:, pl.ds(0, half)], h2.at[:, pl.ds(half, half)]]
    my_mark = tok.at[mark_at(y, c, x)]
    for first in (True, False):
        part_x, part_y = (0, 1) if first else (1, 0)
        for d in near:
            push(0, own[part_x], *slot(part_x, y, x), dev(around(x, d), y, c))
            push(0, own[part_y], *slot(part_y, y, x), dev(x, around(y, d), c))
        if first:
            for d in near:
                push(2, marks, my_mark, t_sem.at[y, x], dev(around(x, d), y, c))
                push(2, marks, my_mark, t_sem.at[y, x], dev(x, around(y, d), c))
            push(0, own[0], hid.at[block_at(0, y, c, x)], hp_sem.at[0, y], partner)
            push(0, own[1], hid.at[block_at(1, y, c, x)], hp_sem.at[1, y], partner)
            push(2, marks, my_mark, tp_sem.at[y], partner)
    for d in near:
        push(3, gate_b.at[around(x, d)], gat.at[RING + x], g_sem.at[1], dev(around(x, d), y, c))
        push(3, gate_a.at[around(y, d)], gat.at[y], g_sem.at[0], dev(x, around(y, d), c))
    hid[block_at(0, y, c, x)] = h2[:, :half]
    hid[block_at(1, y, c, x)] = h2[:, half:]
    tok[mark_at(y, c, x)] = marks[...]
    gat[y] = gate_a[y]
    gat[RING + x] = gate_b[x]

    def onward(part, py, px, steps):
        ref, sem = slot(part, py, px)
        for e in steps:
            push(0, ref, ref, sem, dev(x, around(y, e), c) if part == 0 else dev(around(x, e), y, c))

    for d in near:
        px, py = around(x, d), around(y, d)
        landed(*slot(0, y, px))
        onward(0, y, px, (1, 3))
        to_partner(0, y, px)
        landed(*slot(1, py, x))
        onward(1, py, x, (1, 3))
        to_partner(1, py, x)
        ref = tok.at[mark_at(y, c, px)]
        landed(ref, t_sem.at[y, px])
        for e in near:
            push(2, ref, ref, t_sem.at[y, px], dev(x, around(y, e), c))
        push(2, ref, ref, tp_sem.at[y], partner)
    for d in near:
        onward(0, y, around(x, d), (2,))
        onward(1, around(y, d), x, (2,))
    for d in near:
        px, py = around(x, d), around(y, d)
        landed(*slot(1, y, px))
        to_partner(1, y, px)
        landed(*slot(0, py, x))
        to_partner(0, py, x)

    lane = iota((8, 128), 1)
    strict = jnp.where((iota((128, 128), 0) < iota((128, 128), 1)) & (iota((128, 128), 0) // rows == iota((128, 128), 1) // rows), 1.0, 0.0).astype(BF16)
    quad_seats = RING * seats

    def expert_chunk(step, quads):
        keep = [[], []]
        for q, (off, dc) in enumerate(quads):
            py, pc = around(y, off), (c + dc) % CORES
            first = mark_at(py, pc, 0)
            ids = tok[first] + tok[first + 1] + tok[first + 2] + tok[first + 3]
            hits = []
            for e in range(2):
                match = jnp.where(ids == (me * 2 + e + 1).astype(F32), 1.0, 0.0)
                hits.append(jnp.broadcast_to(jnp.sum(match, axis=0, keepdims=True), (8, 128)))
            rank = dot32((hits[0] + hits[1]).astype(BF16), strict)
            seat = rank + (lane // rows * seats).astype(F32)
            picks = []
            for e in range(2):
                pick = jnp.where((iota((quad_seats, 128), 0).astype(F32) == seat[0:1]) & (hits[e][0:1] > 0.5), 1.0, 0.0)
                keep[e].append(jnp.sum(pick, axis=1, keepdims=True))
                picks.append(pick.astype(BF16))
            pick = jnp.concatenate(picks, axis=0)
            for part in range(2):
                src = hid[pl.ds(block_at(part, py, pc, 0), RING)].reshape(RING * rows, half)
                got = dot32(pick, src).astype(BF16)
                for e in range(2):
                    xs[e, q * quad_seats:(q + 1) * quad_seats, part * half:(part + 1) * half] = got[e * quad_seats:(e + 1) * quad_seats]
        if step == 0:
            loads[0].wait()
            loads[1].wait()
        hidden = []
        block = ff // 2
        for n in range(2):
            cols = slice(n * block, (n + 1) * block)
            a = dot32(xs[0], wg[0, :, cols]) + dot32(xs[1], wg[1, :, cols])
            u = dot32(xs[0], wu[0, :, cols]) + dot32(xs[1], wu[1, :, cols])
            hidden.append((jax.nn.silu(a) * u).astype(BF16))
        act = jnp.concatenate(hidden, axis=1)
        masks = [jnp.concatenate(k, axis=0) for k in keep]
        acts = [jnp.where(m > 0.5, act, jnp.zeros_like(act)) for m in masks]
        if step == 0:
            loads[2].wait()
        for lo, leg in ((half, leg_b), (0, leg_a)):
            for at in range(lo, lo + half, half // 2):
                cols = slice(at, at + half // 2)
                ys[step, :, cols] = (dot32(acts[0], wd[0, :, cols]) + dot32(acts[1], wd[1, :, cols])).astype(BF16)
            for q, (off, dc) in enumerate(quads):
                leg(step, q, off, dc)

    def leg_a(step, q, off, dc):
        py, pc = around(y, off), (c + dc) % CORES
        mine = CORES * x + c
        for dx in (0,) + near:
            px = around(x, dx)
            src = ys.at[step, pl.ds(q * quad_seats + px * seats, seats), pl.ds(0, cut)]
            if dx == 0 and dc == 0:
                r1a[py * RING * CORES + mine] = src[...]
            else:
                push(4, src, r1a.at[py * RING * CORES + mine], r1a_sem.at[py], dev(px, y, pc))

    def leg_b(step, q, off, dc):
        mine = CORES * y + c
        src = ys.at[step, pl.ds(q * quad_seats, quad_seats), pl.ds(cut, rest)]
        if off == 0 and dc == 0:
            r1b[mine] = src[...]
        else:
            push(5, src, r1b.at[mine], r1b_sem.at[0], dev(x, around(y, off), (c + dc) % CORES))

    def weigh(gate, data):
        total = dot32(jnp.concatenate(split3(gate), axis=0), data)
        return total[:rows] + total[rows:2 * rows] + total[2 * rows:]

    def second_leg_a(off):
        py = around(y, off)
        line = RING * CORES
        landed(r1a.at[pl.ds(py * line, line - 1)], r1a_sem.at[py])
        part = weigh(gat[py], r1a[pl.ds(py * line, line)].reshape(line * seats, cut))
        if off:
            sa[py] = part
            push(6, sa.at[py], r2a.at[y], r2_sem.at[0], dev(x, py, c))
        else:
            r2a[y] = part

    def share_row(d):
        qy = around(y, d)
        for e in near:
            qx = around(x, e)
            landed(*slot(0, qy, qx))
            to_partner(0, qy, qx)
            landed(*slot(1, qy, qx))
            to_partner(1, qy, qx)
        for e in range(RING):
            qx = around(x, e)
            ref = tok.at[mark_at(qy, c, qx)]
            landed(ref, t_sem.at[qy, qx])
            push(2, ref, ref, tp_sem.at[qy], partner)

    def partner_row(d):
        qy = around(y, d)
        for part in range(2):
            landed(hid.at[pl.ds(block_at(part, qy, other, 0), RING)], hp_sem.at[part, qy])
        landed(tok.at[pl.ds(mark_at(qy, other, 0), RING)], tp_sem.at[qy])

    partner_row(0)
    expert_chunk(0, ((0, 0), (0, 1)))
    share_row(1)
    share_row(3)
    expert_chunk(1, ((1, 0), (3, 0)))
    share_row(2)
    landed(gat.at[pl.ds(0, RING - 1)], g_sem.at[0])
    landed(gat.at[pl.ds(0, RING - 1)], g_sem.at[1])
    second_leg_a(0)
    partner_row(2)
    expert_chunk(2, ((2, 0), (2, 1)))
    partner_row(1)
    partner_row(3)
    expert_chunk(3, ((1, 1), (3, 1)))
    second_leg_a(2)
    landed(r1b.at[pl.ds(0, RING * CORES - 1)], r1b_sem.at[0])
    for d in (2, 1, 3, 0):
        px = around(x, d)
        data = jnp.concatenate([r1b[k, pl.ds(px * seats, seats), :] for k in range(RING * CORES)], axis=0)
        part = weigh(gat[RING + px], data)
        if d:
            sb[px] = part
            push(7, sb.at[px], r2b.at[x], r2_sem.at[1], dev(px, y, c))
        else:
            r2b[x] = part
    second_leg_a(1)
    second_leg_a(3)
    landed(r2a.at[pl.ds(0, RING - 1)], r2_sem.at[0])
    out[:, :cut] = (x_mid[:, :cut].astype(F32) + ((r2a[0] + r2a[1]) + (r2a[2] + r2a[3]))).astype(BF16)
    landed(r2b.at[pl.ds(0, RING - 1)], r2_sem.at[1])
    out[:, cut:] = (x_mid[:, cut:].astype(F32) + ((r2b[0] + r2b[1]) + (r2b[2] + r2b[3]))).astype(BF16)
    sizes = (hid, hid, tok, gat, r1a, r1b, r2a, r2b)
    for kind, ref in enumerate(sizes):
        if sent[kind]:
            landed(ref.at[pl.ds(0, sent[kind])], send_sem.at[kind])


def exchange(h2, marks, gate_a, gate_b, x_mid, w_gate, w_up, w_down, seats):
    rows, width = h2.shape
    half = width // 2
    cut = width * 5 // 8
    rest = width - cut
    e_local, _, ff = w_gate.shape
    line = RING * CORES
    vmem = pl.BlockSpec(memory_space=pltpu.VMEM)
    hbm = pl.BlockSpec(memory_space=pl.ANY)
    dma = pltpu.SemaphoreType.DMA
    return pl.pallas_call(
        exchange_kernel,
        out_shape=jax.ShapeDtypeStruct((rows, width), BF16),
        in_specs=[vmem] * 5 + [hbm] * 3,
        out_specs=vmem,
        scratch_shapes=[
            pltpu.VMEM((2 * RING * line, rows, half), BF16),
            pltpu.VMEM((RING * line, 8, 128), F32),
            pltpu.VMEM((2 * RING, rows, 128), F32),
            pltpu.VMEM(w_gate.shape, BF16),
            pltpu.VMEM(w_up.shape, BF16),
            pltpu.VMEM(w_down.shape, BF16),
            pltpu.VMEM((e_local, line * seats, width), BF16),
            pltpu.VMEM((RING, line * seats, width), BF16),
            pltpu.VMEM((RING * line, seats, cut), BF16),
            pltpu.VMEM((line, RING * seats, rest), BF16),
            pltpu.VMEM((RING, rows, cut), F32),
            pltpu.VMEM((RING, rows, rest), F32),
            pltpu.VMEM((RING, rows, cut), F32),
            pltpu.VMEM((RING, rows, rest), F32),
            dma((3,)),
            dma((2, RING, RING)),
            dma((2, RING)),
            dma((RING, RING)),
            dma((RING,)),
            dma((2,)),
            dma((RING,)),
            dma((1,)),
            dma((2,)),
            dma((8,)),
        ],
        compiler_params=pltpu.CompilerParams(collective_id=0, has_side_effects=True, vmem_limit_bytes=60 * 2 ** 20),
        name='exchange',
    )(h2, marks, gate_a, gate_b, x_mid, w_gate, w_up, w_down)


def solution(mesh):
    row_spec = P(('dp', 'ep'))
    rep = P()
    expert_spec = P('ep')
    in_specs = (row_spec,) * 5 + (rep,) * 9 + (expert_spec,) * 3

    def device_step(x_in, k_cache, v_cache, cache_len, topk_idx, ln_attn, w_q, w_k, w_v, q_norm, k_norm, w_o, ln_moe, w_router, w_gate, w_up, w_down):
        rows, top_k = topk_idx.shape
        seats = 2 * rows * top_k // mesh.shape['ep']
        k_full, v_full, x_mid, h2, gate_a, gate_b, marks = attend(x_in, k_cache, v_cache, cache_len, topk_idx, ln_attn, w_q, w_k, w_v, q_norm, k_norm, w_o, ln_moe, w_router)
        x_out = exchange(h2, marks, gate_a, gate_b, x_mid, w_gate, w_up, w_down, seats)
        return x_out, k_full, v_full

    return jax.shard_map(device_step, mesh=mesh, in_specs=in_specs, out_specs=(row_spec,) * 3, check_vma=False)
```

time: 97.2 us -> 76.7 us (0.79)
  matrix products: 19.7 us -> 0 us
  Pallas kernels: 62 us -> 74.3 us
  other arithmetic: 6.79 us -> 0 us
  local copies, waits for them, and re-layouts: 7.66 us -> 1.57 us
    dot_general x6 -> x0, matrix products: 19.7 us -> none  [the longest x1 5.64 us: attend_block(): jnp.dot(attn_out, w_o, preferred_element_type=jnp.float32)]
    pallas_call x1, Pallas kernels: 2.57 us -> 19.9 us  [attend(): pl.pallas_call(attend_kernel, out_shape=(jax.ShapeDtypeStruct(k_cache.sha...]
    unnamed x34 -> x1, local copies, waits for them, and re-layouts: 7.06 us -> 1.57 us
    pallas_call x1, Pallas kernels: 59.4 us -> 54.4 us  [exchange(): pl.pallas_call(exchange_kernel, out_shape=jax.ShapeDtypeStruct((rows, wid...]
    select_n x1 -> x0, other arithmetic: 2.97 us -> none  [attend_block(): k_full = jnp.where(is_new, k_new[:, None], k_cache)]
    reduce_sum x3 -> x0, other arithmetic: 1.77 us -> none  [norm_scale(): jnp.mean(values * values, axis=-1, keepdims=True) + NORM_EPS]
where the time goes in v2:
time: 76.7 us; the launch traced here: 76.5 us
  Pallas kernels  74.3 us (97%)
  local copies, waits for them, and re-layouts  1.57 us (2%)
    pallas_call x1, Pallas kernels, exchange(): pl.pallas_call(exchange_kernel, out_shape=jax.ShapeDtypeStruct((rows, wid...  54.4 us
    pallas_call x1, Pallas kernels, attend(): pl.pallas_call(attend_kernel, out_shape=(jax.ShapeDtypeStruct(k_cache.sha...  19.9 us
    unnamed x1, local copies, waits for them, and re-layouts  1.57 us

profile of v2, /device:TPU:97, one launch (start us, length us, event | category | flops | bytes accessed | tf_op | source)
XLA Modules:
  0.0 76.5 jit_solution(2232353579921290518)
XLA Ops:
  0.6 19.9 %attend.1 = (bf16[32,32,16,128]{3,2,1,0:T(8,128)(2,1)}, bf16[32,32,16,128]{3,2,1,0:T(8,128)(2,1)}, bf16[32,2048]{1,0:T(8,128)(2,1)}, bf16[32,2048]{1,0:T(8,128)(...) custom-call(s32[32]{0:T(128)} %lens.1, bf16[32,2048]{1,0:T(8,128)(2,1)} %x_in.1, ...), custom_call_target="tpu_custom_call" | custom-call | tf_op jit(solution)/shard_map/attend/pallas_call | solution.py:218
  20.5 54.4 %exchange.1 = bf16[32,2048]{1,0:T(8,128)(2,1)} custom-call(bf16[32,2048]{1,0:T(8,128)(2,1)} %get-tuple-element.10.h2, f32[8,128]{1,0:T(8,128)} %get-tuple-element.11.marks, f32[4,32,128]{2,1,0:T(8,128)} %get-tuple-element.12.gate_a, f32[4,32,128]{2,1,0:T(8,128)} %get-tuple-element.13.gate_b, bf16[32,2048]{1,0:T(8,128)(2,1)} %get-tuple-element.14.x_mid, ...), custom_call_target="tpu_custom_call" | custom-call | tf_op jit(solution)/shard_map/exchange/pallas_call | solution.py:510
  74.9 1.6 %copy.21 = bf16[32,2048]{1,0:T(8,128)(2,1)} copy(bf16[32,2048]{1,0:T(8,128)(2,1)} %exchange.1) | data formatting | bytes 262144
